TPU v7x, 128 devices: a whole 4x4x4 slice. The times are simulated.
128 devices in a mesh: fsdp: 8 (over x_lo, y), seq: 16 (over x_hi, z, core).
Axes of the slice: x: 4 (x_hi: 2, x_lo: 2; x = x_hi * 2 + x_lo), y: 4, z: 4, core: 2. Of those that a mesh axis runs over, the one named last changes fastest.
Arguments:
- image_input: bfloat16 [8, 2048, 1536], P('fsdp', 'seq'), may hold values from -6 to 6
- text_input: bfloat16 [8, 128, 1536], P('fsdp'), may hold values from -6 to 6
- w_qkv: bfloat16 [1536, 3, 2048], P('fsdp'), may hold values from -0.15625 to 0.15625
- query_gain: float32 [128], replicated, may hold values from 1.2 to 2.4
- key_gain: float32 [128], replicated, may hold values from 1.2 to 2.4
- image_cotangent: bfloat16 [8, 2048, 2048], P('fsdp', 'seq'), may hold values from -6 to 6
- text_cotangent: bfloat16 [8, 128, 2048], P('fsdp'), may hold values from -6 to 6
Outputs:
- image_grad: bfloat16 [8, 2048, 1536], P('fsdp', 'seq')
- text_grad: bfloat16 [8, 128, 1536], P('fsdp')
- weight_grad: float32 [1536, 3, 2048], P('fsdp', None, 'seq')
- gain_grad: float32 [2, 128], replicated
All inputs are finite; a program needn't handle non-finite values.
Results may differ from a plain program's by a relative error of at most 0.018.
The roundings to bfloat16 on the way count: a program that leaves them out, or rounds other values in their place, can miss the bound.
Values may be sent and summed in bfloat16 or wider, within the bound.
A program may use at most 192 MiB of HBM per device.

v0:
```python
import math

import jax
import jax.numpy as jnp
from jax import lax
from jax.sharding import Mesh
from jax.sharding import PartitionSpec as P

HEADS = 16
HEAD = 128
SEQ = ("seq_0", "seq_1", "seq_2")
FSDP = ("fsdp_0", "fsdp_1")
FSDP_SEQ = ("fsdp_0", "fsdp_1", "seq_0", "seq_1", "seq_2")


epsilon = 1e-06
query_parts = 4


def over_axes(shard, axes):
    for axis in axes:
        shard = lax.psum(shard, axis)
    return shard


def sent_to_all(shard, axis):
    copies = jnp.broadcast_to(shard, (lax.axis_size(axis), *shard.shape))
    return lax.all_to_all(copies, axis, split_axis=0, concat_axis=0, tiled=True)


def in_order(pieces, dim):
    pieces = jnp.moveaxis(pieces, 0, dim)
    lengths = pieces.shape
    return pieces.reshape(*lengths[:dim], lengths[dim] * lengths[dim + 1], *lengths[dim + 2 :])


def collect(shard, axis, dim):
    pieces = sent_to_all(shard, axis)
    return in_order(pieces, dim)


def rms_forward(values, gain):
    floated = values.astype(jnp.float32)
    inverse = lax.rsqrt(jnp.mean(floated * floated, axis=-1, keepdims=True) + epsilon)
    return (floated, inverse, (floated * inverse * gain).astype(jnp.bfloat16))


def rms_backward(floated, inverse, gain, incoming):
    weighted = incoming * gain
    inner_mean = jnp.mean(weighted * floated, axis=-1, keepdims=True)
    grad_input = inverse * weighted - floated * inverse * inverse * inverse * inner_mean
    grad_gain = jnp.sum(incoming * floated * inverse, axis=0)
    return (grad_input, grad_gain)


def head_backward(query_rows, key_rows, value_rows, incoming, query_gain, key_gain):
    query_float, query_inverse, query_normed = rms_forward(query_rows, query_gain)
    key_float, key_inverse, key_normed = rms_forward(key_rows, key_gain)
    length = query_rows.shape[0]
    width = query_rows.shape[1]
    block_rows = length // query_parts
    factor = 1.0 / math.sqrt(width)
    query_blocks = query_normed.reshape(query_parts, block_rows, width)
    incoming_blocks = incoming.reshape(query_parts, block_rows, width)

    def visit(carried, pieces):
        key_total, value_total = carried
        query_piece, incoming_piece = pieces
        scores = jnp.dot(query_piece, key_normed.T, preferred_element_type=jnp.float32) * factor
        attention = jax.nn.softmax(scores, axis=-1)
        attention_grad = jnp.dot(incoming_piece, value_rows.T, preferred_element_type=jnp.float32)
        row_dot = jnp.sum(attention * attention_grad, axis=-1, keepdims=True)
        score_grad = (attention * (attention_grad - row_dot)).astype(jnp.bfloat16)
        value_total = value_total + jnp.dot(
            attention.astype(jnp.bfloat16).T, incoming_piece, preferred_element_type=jnp.float32
        )
        key_total = (
            key_total
            + jnp.dot(score_grad.T, query_piece, preferred_element_type=jnp.float32) * factor
        )
        query_grad = jnp.dot(score_grad, key_normed, preferred_element_type=jnp.float32) * factor
        return ((key_total, value_total), query_grad)

    zeros_init = jnp.zeros((length, width), jnp.float32)
    (key_total, value_total), query_pieces = lax.scan(
        visit, (zeros_init, zeros_init), (query_blocks, incoming_blocks)
    )
    query_grad = query_pieces.reshape(length, width)
    query_input_grad, query_gain_grad = rms_backward(
        query_float, query_inverse, query_gain, query_grad
    )
    key_input_grad, key_gain_grad = rms_backward(key_float, key_inverse, key_gain, key_total)
    stacked = jnp.stack([query_input_grad, key_input_grad, value_total], axis=1).astype(
        jnp.bfloat16
    )
    return (stacked, jnp.stack([query_gain_grad, key_gain_grad], axis=0))


def local(image_input, text_input, w_qkv, query_gain, key_gain, image_cotangent, text_cotangent):
    member_count = lax.axis_size(SEQ)
    own_index = lax.axis_index(SEQ)
    local_heads = HEADS // member_count
    own_width = local_heads * HEAD
    offset = own_index * own_width
    text_length = text_input.shape[1]
    image_rows_dev = image_input.shape[1]
    weights = lax.all_gather(w_qkv, FSDP, axis=0, tiled=True)
    image_triple = jnp.einsum(
        "btd,dch->btch", image_input, weights, preferred_element_type=jnp.float32
    ).astype(jnp.bfloat16)
    stacked = jnp.concatenate([image_triple, image_cotangent[:, :, None, :]], axis=2)
    arrived = lax.all_to_all(stacked, SEQ, split_axis=3, concat_axis=1, tiled=True)
    own_weights = lax.dynamic_slice_in_dim(weights, offset, own_width, 2)
    text_triple = jnp.einsum(
        "btd,dch->btch", text_input, own_weights, preferred_element_type=jnp.float32
    ).astype(jnp.bfloat16)
    text_incoming = lax.dynamic_slice_in_dim(text_cotangent, offset, own_width, 2)
    joined_triple = jnp.concatenate([text_triple, arrived[:, :, :3]], axis=1)
    joined_incoming = jnp.concatenate([text_incoming, arrived[:, :, 3]], axis=1)
    batch_rows = joined_triple.shape[0]
    length = joined_triple.shape[1]
    split_triple = joined_triple.reshape(batch_rows, length, 3, local_heads, HEAD)
    split_incoming = joined_incoming.reshape(batch_rows, length, local_heads, HEAD)
    per_head = jax.vmap(head_backward, in_axes=(1, 1, 1, 1, None, None), out_axes=(2, 0))
    per_batch = jax.vmap(per_head, in_axes=(0, 0, 0, 0, None, None), out_axes=(0, 0))
    head_grads, gain_parts = per_batch(
        split_triple[:, :, 0],
        split_triple[:, :, 1],
        split_triple[:, :, 2],
        split_incoming,
        query_gain,
        key_gain,
    )
    head_grads = head_grads.reshape(batch_rows, length, 3, own_width)
    text_grads = head_grads[:, :text_length]
    image_grads = head_grads[:, text_length:]
    gain_total = over_axes(jnp.sum(gain_parts, axis=(0, 1)), FSDP_SEQ)
    image_tokens, text_share = (
        lax.all_to_all(image_grads, SEQ, split_axis=1, concat_axis=3, tiled=True),
        lax.all_to_all(text_grads, SEQ, split_axis=1, concat_axis=3, tiled=True),
    )
    text_piece = jnp.einsum(
        "btch,dch->btd", text_share, weights, preferred_element_type=jnp.float32
    ).astype(jnp.bfloat16)
    text_out = collect(text_piece, SEQ, 1)
    image_out = jnp.einsum(
        "btch,dch->btd", image_tokens, weights, preferred_element_type=jnp.float32
    ).astype(jnp.bfloat16)
    text_part = jnp.einsum(
        "btd,btch->dch", text_input, text_grads, preferred_element_type=jnp.float32
    )
    whole_image = lax.all_gather(image_input, SEQ, axis=1, tiled=True)

    def add_block(block, running):
        start = (block * image_rows_dev).astype(jnp.int32)
        image_block = lax.dynamic_slice_in_dim(whole_image, start, image_rows_dev, 1)
        grad_block = lax.dynamic_slice_in_dim(image_grads, start, image_rows_dev, 1)
        selected = (block == own_index).astype(jnp.float32)
        term = (
            jnp.einsum("btd,btch->dch", image_block, grad_block, preferred_element_type=jnp.float32)
            + text_part * selected
        )
        rounded = lax.optimization_barrier(term.astype(jnp.bfloat16))
        return running + rounded.astype(jnp.float32)

    start_total = jnp.zeros((image_input.shape[2], 3, own_width), jnp.float32)
    head_total = lax.fori_loop(0, member_count, add_block, start_total)
    grad_weights = lax.psum_scatter(
        head_total.astype(jnp.bfloat16), FSDP, scatter_dimension=0, tiled=True
    ).astype(jnp.float32)
    return (image_out, text_out, grad_weights, gain_total)


def solution(mesh):
    finer = Mesh(
        mesh.devices.reshape(2, 4, 2, 4, 2), ("fsdp_0", "fsdp_1", "seq_0", "seq_1", "seq_2")
    )
    return jax.shard_map(
        local,
        mesh=finer,
        in_specs=(
            P(FSDP, SEQ, None),
            P(FSDP, None, None),
            P(FSDP, None, None),
            P(),
            P(),
            P(FSDP, SEQ, None),
            P(FSDP, None, None),
        ),
        out_specs=(P(FSDP, SEQ, None), P(FSDP, None, None), P(FSDP, None, SEQ), P()),
        check_vma=False,
    )
```

profile of v0, /device:TPU:1, one launch (start us, length us, event | category | flops | bytes accessed | tf_op | source)
XLA Modules:
  0.0 568.3 jit_solution(10059944847568096801)
XLA Ops:
  8.8 194.9 %all-gather.3.cloned.1.call-done = bf16[1536,3,2048]{2,0,1:T(8,128)(2,1)} async-done(((bf16[192,3,2048]{2,0,1:T(8,128)(2,1)}), bf16[1536,3,2048]{2,0,1:T(8,128)(2,1)}) %all-gather.3.cloned.1.call-update) | async-done | bytes 18874384 | tf_op jit(solution)/shard_map/all_gather | solution.py:107
  203.7 9.0 %fusion.31 = bf16[1,128,3,2048]{3,1,2,0:T(8,128)(2,1)S(1)} fusion(bf16[1536,3,2048]{2,0,1:T(8,128)(2,1)} %all-gather.3.cloned.1.call-done, bf16[1,128,1536]{2,1,0:T(8,128)(2,1)S(1)} %copy-done.15), kind=kOutput, calls=%fused_computation.41 | convolution fusion | flops 2416705536 | bytes 20840448 | tf_op jit(solution)/shard_map/btd,dch->btch/dot_general | solution.py:108
  212.9 2.6 copy.49
  215.5 7.4 %all-to-all-start = ((bf16[1,128,4,2048]{1,2,0,3:T(4,128)(2,1)}), bf16[1,128,4,2048]{1,2,0,3:T(4,128)(2,1)}, u32[]{:S(2)}, u32[]{:S(2)}) async-start(bf16[1,128,4,2048]{1,2,0,3:T(4,128)(2,1)} %copy.49), calls=%async_computation | async-start | bytes 4194304 | tf_op jit(solution)/shard_map/all_to_all | solution.py:112
  225.9 29.6 %all-to-all-done = bf16[1,128,4,2048]{1,2,0,3:T(4,128)(2,1)} async-done(((bf16[1,128,4,2048]{1,2,0,3:T(4,128)(2,1)}), bf16[1,128,4,2048]{1,2,0,3:T(4,128)(2,1)}, u32[]{:S(2)}, u32[]{:S(2)}) %all-to-all-start) | async-done | bytes 2097184 | tf_op jit(solution)/shard_map/all_to_all | solution.py:112
  255.5 4.3 copy.80
  259.8 4.2 all_to_all.41
  268.2 2.9 copy.52
  281.7 71.7 %while.29 = (s32[]{:T(128)}, f32[1,1,2176,128]{3,2,1,0:T(8,128)S(1)}, f32[1,1,2176,128]{3,2,1,0:T(8,128)}, f32[4,1,1,544,128]{4,3,2,1,0:T(8,128)}, bf16[4,1,1,54...) while((s32[]{:T(128)}, ...), condition=%wide.region_6.7_spmd.clone, body=%wide.region_2.6_spmd.clone.sunk | while | flops 1535592832 | bytes 89573472 | solution.py:85
  286.7 4.8 fusion.106
  304.3 5.1 fusion.106
  322.4 5.2 fusion.106
  327.5 2.4 multiply_reduce_fusion.3
  340.4 5.1 fusion.106
  354.9 2.7 copy.70
  359.3 2.7 copy.59
  369.6 7.2 %all-to-all-start.2 = ((bf16[1,128,3,128]{3,2,0,1:T(4,128)(2,1)}), bf16[1,128,3,128]{3,2,0,1:T(4,128)(2,1)S(1)}, u32[]{:S(2)}, u32[]{:S(2)}) async-start(bf16[1,128,3,128]{3,2,0,1:T(4,128)(2,1)} %copy.65), calls=%async_computation.2 | async-start | bytes 262144 | tf_op jit(solution)/shard_map/all_to_all | solution.py:140
  379.3 5.1 all-to-all-done.2
  384.4 9.0 %fusion.34 = bf16[8,1536]{1,0:T(8,128)(2,1)S(1)} fusion(bf16[1536,3,2048]{2,0,1:T(8,128)(2,1)} %all-gather.3.cloned.1.call-done, bf16[1,128,3,128]{3,2,0,1:T(4,128)(2,1)S(1)} %all-to-all-done.2), kind=kOutput, calls=%fused_computation.46 | convolution fusion | flops 151007232 | bytes 18997248 | tf_op jit(solution)/shard_map/btch,dch->btd/dot_general | solution.py:142
  394.2 4.0 all-to-all-start.3
  398.6 2.5 copy.63
  401.1 6.9 %all-to-all-done.3 = bf16[16,1,8,1536]{3,2,1,0:T(8,128)(2,1)S(1)} async-done(((bf16[16,1,8,1536]{3,2,1,0:T(8,128)(2,1)}), bf16[16,1,8,1536]{3,2,1,0:T(8,128)(2,1)S(1)}, u32[]{:S(2)}, u32[]{:S(2)}) %all-to-all-start.3) | async-done | bytes 393248 | tf_op jit(solution)/shard_map/all_to_all | solution.py:28
  408.8 5.4 all-to-all-start.1
  414.3 87.6 %while.30 = (s32[]{:T(128)}, f32[1536,3,128]{2,0,1:T(8,128)}, bf16[1,2048,1536]{1,2,0:T(8,128)(2,1)}, bf16[1,2048,3,128]{1,3,2,0:T(8,128)(2,1)S(1)}, s32[]{:T(12...) while((s32[]{:T(128)}, f32[1536,3,128]{2,0,1:T(8,128)}, ...), condition=%wide.region_10.11_spmd.clone, body=%wide.region_9.10_spmd.clone.sunk | while | flops 154533888 | bytes 9930411 | solution.py:167
  420.5 3.3 select_add_fusion.2
  426.1 3.3 select_add_fusion.2
  431.7 3.3 select_add_fusion.2
  437.2 3.3 select_add_fusion.2
  442.8 3.3 select_add_fusion.2
  448.4 3.3 select_add_fusion.2
  454.0 3.3 select_add_fusion.2
  459.5 3.3 select_add_fusion.2
  465.1 3.3 select_add_fusion.2
  470.7 3.3 select_add_fusion.2
  476.3 3.3 select_add_fusion.2
  481.9 3.3 select_add_fusion.2
  487.4 3.3 select_add_fusion.2
  493.0 3.3 select_add_fusion.2
  498.6 3.3 select_add_fusion.2
  501.9 2.8 convert_element_type.211
  504.8 3.8 psum.35
  508.6 6.1 %psum.36 = f32[2,128]{1,0:T(2,128)S(1)} all-reduce(f32[2,128]{1,0:T(2,128)S(1)} %psum.35), channel_id=1, replica_groups=mesh['fsdp_0'=2,'fsdp_1'=4,'seq_0'=2,'seq_1'=4,'seq_2'=2] {'fsdp_1'}, use_global_device_ids=true, to_apply=%region_15.16 | all-reduce | flops 256 | bytes 2048 | tf_op jit(solution)/shard_map/psum | solution.py:22
  514.7 5.7 psum.37
  520.4 9.2 %psum.38 = f32[2,128]{1,0:T(2,128)S(1)} all-reduce(f32[2,128]{1,0:T(2,128)S(1)} %psum.37), channel_id=1, replica_groups=mesh['fsdp_0'=2,'fsdp_1'=4,'seq_0'=2,'seq_1'=4,'seq_2'=2] {'seq_1'}, use_global_device_ids=true, to_apply=%region_17.18 | all-reduce | flops 256 | bytes 2048 | tf_op jit(solution)/shard_map/psum | solution.py:22
  529.6 8.8 %psum.39 = f32[2,128]{1,0:T(2,128)} all-reduce(f32[2,128]{1,0:T(2,128)S(1)} %psum.38), channel_id=1, replica_groups=mesh['fsdp_0'=2,'fsdp_1'=4,'seq_0'=2,'seq_1'=4,'seq_2'=2] {'seq_2'}, use_global_device_ids=true, to_apply=%region_18.19 | all-reduce | flops 256 | bytes 2048 | tf_op jit(solution)/shard_map/psum | solution.py:22
  538.3 4.0 copy.81
  542.4 2.5 reshape.756
  545.0 13.5 %fusion.33 = bf16[1,128,1536]{2,1,0:T(8,128)(2,1)} fusion(bf16[128,3,2048]{2,0,1:T(8,128)(2,1)S(1)} %reshape.756, bf16[1536,3,2048]{2,0,1:T(8,128)(2,1)} %all-gather.3.cloned.1.call-done), kind=kOutput, calls=%fused_computation.44 | convolution fusion | flops 2416115712 | bytes 20840448 | tf_op jit(solution)/shard_map/btch,dch->btd/dot_general | solution.py:146
  (164 shorter events, 123.1 us)
Async XLA Ops:
  8.0 216.0 %copy-start = (bf16[1,128,2048]{2,1,0:T(8,128)(2,1)S(1)}, bf16[1,128,2048]{2,1,0:T(8,128)(2,1)}, u32[]{:S(2)}) copy-start(bf16[1,128,2048]{2,1,0:T(8,128)(2,1)} %param.17) | copy-start | bytes 1572868
  8.0 195.7 %copy-start.15 = (bf16[1,128,1536]{2,1,0:T(8,128)(2,1)S(1)}, bf16[1,128,1536]{2,1,0:T(8,128)(2,1)}, u32[]{:S(2)}) copy-start(bf16[1,128,1536]{2,1,0:T(8,128)(2,1)} %param.11) | copy-start | bytes 1179652
  8.0 195.7 %all-gather.3.cloned.1.call-start = ((), (), s32[]{:S(2)}) async-start(), calls=%async_computation.5 | async-start | bytes 21233664 | tf_op jit(solution)/shard_map/all_gather | solution.py:107
  8.8 203.9 %copy-start.21 = (bf16[1,128,2048]{2,1,0:T(8,128)(2,1)S(1)}, bf16[1,128,2048]{2,1,0:T(8,128)(2,1)}, u32[]{:S(2)}) copy-start(bf16[1,128,2048]{2,1,0:T(8,128)(2,1)} %param.16) | copy-start | bytes 1572868
  215.5 40.0 %all-to-all-start = ((bf16[1,128,4,2048]{1,2,0,3:T(4,128)(2,1)}), bf16[1,128,4,2048]{1,2,0,3:T(4,128)(2,1)}, u32[]{:S(2)}, u32[]{:S(2)}) async-start(bf16[1,128,4,2048]{1,2,0,3:T(4,128)(2,1)} %copy.49), calls=%async_computation | async-start | bytes 4194304 | tf_op jit(solution)/shard_map/all_to_all | solution.py:112
  222.9 1.2 copy-start.18
  222.9 191.3 %all-gather.5.cloned.1.call-start = ((), (), s32[]{:S(2)}) async-start(), calls=%async_computation.6 | async-start | bytes 6684672 | tf_op jit(solution)/shard_map/all_gather | solution.py:152
  264.0 1.4 slice-start
  265.8 2.2 copy-start.7
  268.0 3.1 copy-start.22
  274.2 5.1 copy-start.23
  283.7 2.2 copy-start.2
  286.7 4.8 copy-start.3
  286.7 4.8 copy-start.20
  295.4 2.4 copy-start.4
  301.4 2.2 copy-start.2
  304.3 5.2 copy-start.3
  304.3 5.2 copy-start.20
  313.4 2.4 copy-start.4
  319.4 2.2 copy-start.2
  322.3 5.2 copy-start.3
  322.4 5.2 copy-start.20
  331.5 2.4 copy-start.4
  337.4 2.2 copy-start.2
  340.4 5.2 copy-start.3
  340.4 5.2 copy-start.20
  349.5 2.4 copy-start.4
  354.9 2.7 copy-start.5
  359.3 5.0 copy-start.6
  366.2 1.2 copy-start.14
  367.4 0.8 copy-start.10
  367.4 1.3 copy-start.8
  367.8 0.8 copy-start.12
  367.8 9.0 %copy-start.19 = (bf16[1,128,1536]{2,1,0:T(8,128)(2,1)S(1)}, bf16[1,128,1536]{2,1,0:T(8,128)(2,1)}, u32[]{:S(2)}) copy-start(bf16[1,128,1536]{2,1,0:T(8,128)(2,1)} %param.12) | copy-start | bytes 1179652
  369.6 14.8 %all-to-all-start.2 = ((bf16[1,128,3,128]{3,2,0,1:T(4,128)(2,1)}), bf16[1,128,3,128]{3,2,0,1:T(4,128)(2,1)S(1)}, u32[]{:S(2)}, u32[]{:S(2)}) async-start(bf16[1,128,3,128]{3,2,0,1:T(4,128)(2,1)} %copy.65), calls=%async_computation.2 | async-start | bytes 262144 | tf_op jit(solution)/shard_map/all_to_all | solution.py:140
  384.4 13.8 %copy-start.13 = (bf16[1,2176,1,128]{1,3,2,0:T(8,128)(2,1)S(1)}, bf16[1,2176,1,128]{1,3,2,0:T(8,128)(2,1)}, u32[]{:S(2)}) copy-start(bf16[1,2176,1,128]{1,3,2,0:T(8,128)(2,1)} %copy-done.12) | copy-start | bytes 1671172
  393.4 4.8 copy-start.9
  393.4 4.8 copy-start.11
  394.2 13.9 %all-to-all-start.3 = ((bf16[16,1,8,1536]{3,2,1,0:T(8,128)(2,1)}), bf16[16,1,8,1536]{3,2,1,0:T(8,128)(2,1)S(1)}, u32[]{:S(2)}, u32[]{:S(2)}) async-start(bf16[16,1,8,1536]{3,2,1,0:T(8,128)(2,1)} %broadcast_in_dim.17), calls=%async_computation.3 | async-start | bytes 786432 | tf_op jit(solution)/shard_map/all_to_all | solution.py:28
  408.0 0.7 copy-start.16
  408.8 129.6 %all-to-all-start.1 = ((bf16[1,2048,3,128]{3,2,0,1:T(4,128)(2,1)}), bf16[1,2048,3,128]{3,2,0,1:T(4,128)(2,1)}, u32[]{:S(2)}, u32[]{:S(2)}) async-start(bf16[1,2048,3,128]{3,2,0,1:T(4,128)(2,1)} %copy.63), calls=%async_computation.1 | async-start | bytes 4194304 | tf_op jit(solution)/shard_map/all_to_all | solution.py:139
  414.2 144.3 %reduce-scatter.2.cloned.1.call-start = ((), (), s32[]{:S(2)}) async-start(), calls=%async_computation.7 | async-start | bytes 1327104 | tf_op jit(solution)/shard_map/reduce_scatter | solution.py:168
  544.9 15.2 %copy-start.17 = (bf16[16,1,8,1536]{3,2,1,0:T(8,128)(2,1)S(1)}, bf16[16,1,8,1536]{3,2,1,0:T(8,128)(2,1)}, u32[]{:S(2)}) copy-start(bf16[16,1,8,1536]{3,2,1,0:T(8,128)(2,1)} %copy-done.16) | copy-start | bytes 1179652
  544.9 15.9 %copy-start.1 = (bf16[1,128,2048]{2,1,0:T(8,128)(2,1)S(1)}, bf16[1,128,2048]{2,1,0:T(8,128)(2,1)}, u32[]{:S(2)}) copy-start(bf16[1,128,2048]{2,1,0:T(8,128)(2,1)} %param.17) | copy-start | bytes 1572868
Sparse Core Ops, SparseCore 0:
  10.5 193.1 all-gather.2
  504.9 33.6 reduce-scatter.1
Sparse Core Ops, SparseCore 1:
  226.2 74.2 all-gather.4
where the time goes:
time: 571 us; the launch traced here: 568 us
  waiting for transfers between devices  237 us (42%)
  matrix products  124 us (22%)
  other arithmetic  74.9 us (13%)
  local copies, waits for them, and re-layouts  58.3 us (10%)
  blocking collectives  33.6 us (6%)
  starting transfers between devices  24.2 us (4%)
  between operations  15.8 us (3%)
    all_gather x1, waiting for transfers between devices, local(): weights = lax.all_gather(w_qkv, FSDP, axis=0, tiled=True)  195 us
    add x16, other arithmetic, add_block(): return running + rounded.astype(jnp.float32)  50.8 us
    dot_general x16, matrix products, add_block(): jnp.einsum('btd,btch->dch', image_block, grad_block, preferred_element_ty...  36.6 us
    psum x5, blocking collectives, over_axes(): shard = lax.psum(shard, axis)  33.6 us
    all_to_all x1, waiting for transfers between devices, local(): lax.all_to_all(stacked, SEQ, split_axis=3, concat_axis=1, tiled=True)  29.6 us
    dot_general x4, matrix products, visit(): jnp.dot(attention.astype(jnp.bfloat16).T, incoming_piece, preferred_eleme...  20.2 us
    dot_general x1, matrix products, local(): jnp.einsum('btch,dch->btd', image_tokens, weights, preferred_element_type...  13.5 us
    unnamed x46, local copies, waits for them, and re-layouts  11.6 us
  transfers between devices with their start and end apart: 7, of which 4 were waited for; matrix products, arithmetic and copies ran while one was open for 40% of the time, Pallas kernels for 0%

commit v1 on v0

v1 whole, which is shorter than its diff:
```python
import math

import jax
import jax.numpy as jnp
from jax import lax
from jax.experimental import pallas as pl
from jax.experimental.pallas import tpu as pltpu
from jax.sharding import Mesh
from jax.sharding import PartitionSpec as P

HEADS = 16
HEAD = 128
SEQ = ("seq_0", "seq_1", "seq_2")
FSDP = ("fsdp_0", "fsdp_1")
FSDP_SEQ = ("fsdp_0", "fsdp_1", "seq_0", "seq_1", "seq_2")
EPS = 1e-06
F32 = jnp.float32
BF16 = jnp.bfloat16

Q_ROWS = 256
KEY_ROWS = 136


def dot_nt(a, b):
    return lax.dot_general(a, b, (((1,), (1,)), ((), ())), preferred_element_type=F32)


def dot_nn(a, b):
    return lax.dot_general(a, b, (((1,), (0,)), ((), ())), preferred_element_type=F32)


def folded(values):
    rows, width = values.shape
    return jnp.sum(values.reshape(rows // 8, 8, width), axis=0)


def attention_kernel(
    triple, upstream, qgain, kgain, grads, gains, qn, kn, kn_t, expd, dpd, dsd, dk, dv, gsum
):
    rows = triple.shape[0]
    factor = 1.0 / math.sqrt(HEAD)
    scale = factor * math.log2(math.e)

    def normed(values, gain):
        floated = values.astype(F32)
        inverse = lax.rsqrt(jnp.mean(floated * floated, axis=-1, keepdims=True) + EPS)
        return floated, inverse, (floated * inverse * gain).astype(BF16)

    qn[...] = normed(triple[:, 0:HEAD], qgain[...])[2]
    keys = normed(triple[:, HEAD : 2 * HEAD], kgain[...])[2]
    kn[...] = keys
    kn_t[...] = keys.T
    dk[...] = jnp.zeros_like(dk)
    dv[...] = jnp.zeros_like(dv)
    gsum[...] = jnp.zeros_like(gsum)

    def back(values, gain, incoming):
        floated = values.astype(F32)
        inverse = lax.rsqrt(jnp.mean(floated * floated, axis=-1, keepdims=True) + EPS)
        weighted = incoming * gain
        inner = jnp.mean(weighted * floated, axis=-1, keepdims=True)
        grad = inverse * weighted - floated * (inverse * inverse * inverse * inner)
        return grad, folded(incoming * floated * inverse)

    def block(start, count):
        qb = qn[pl.ds(start, count), :]
        ub = upstream[pl.ds(start, count), :]
        total = jnp.zeros((8, count), F32)
        inner = jnp.zeros((8, count), F32)
        for c in range(0, rows, KEY_ROWS):
            part = pl.ds(c, KEY_ROWS)
            e = jnp.exp2(dot_nt(kn[part, :], qb) * scale)
            d = dot_nt(triple[part, 2 * HEAD : 3 * HEAD], ub)
            expd[part, :count] = e
            dpd[part, :count] = d
            total = total + folded(e)
            inner = inner + folded(e * d)
        recip = 1.0 / jnp.sum(total, axis=0, keepdims=True)
        delta = jnp.sum(inner, axis=0, keepdims=True) * recip
        for c in range(0, rows, KEY_ROWS):
            part = pl.ds(c, KEY_ROWS)
            p = expd[part, :count] * recip
            ds = (p * (dpd[part, :count] - delta)).astype(BF16)
            dsd[part, :count] = ds
            dv[part, :] += dot_nn(p.astype(BF16), ub)
            dk[part, :] += dot_nn(ds, qb)
        dq_t = dot_nn(kn_t[...], dsd[:, :count])
        dq = dq_t.T * factor
        grad, gain_part = back(triple[pl.ds(start, count), 0:HEAD], qgain[...], dq)
        grads[pl.ds(start, count), 0:HEAD] = grad.astype(BF16)
        gsum[0:8, :] += gain_part

    image_rows = rows // Q_ROWS * Q_ROWS

    def step(i, carry):
        block(pl.multiple_of(i * Q_ROWS, Q_ROWS), Q_ROWS)
        return carry

    lax.fori_loop(0, image_rows // Q_ROWS, step, 0)
    if rows > image_rows:
        block(image_rows, rows - image_rows)
    grad, gain_part = back(triple[:, HEAD : 2 * HEAD], kgain[...], dk[...] * factor)
    grads[:, HEAD : 2 * HEAD] = grad.astype(BF16)
    grads[:, 2 * HEAD : 3 * HEAD] = dv[...].astype(BF16)
    gsum[8:16, :] = gain_part
    gains[0:1, :] = jnp.sum(gsum[0:8, :], axis=0, keepdims=True)
    gains[1:2, :] = jnp.sum(gsum[8:16, :], axis=0, keepdims=True)


def attention(triple, upstream, query_gain, key_gain):
    rows = triple.shape[0]
    vmem = pl.BlockSpec(memory_space=pltpu.VMEM)
    return pl.pallas_call(
        attention_kernel,
        out_shape=(
            jax.ShapeDtypeStruct((rows, 3 * HEAD), BF16),
            jax.ShapeDtypeStruct((2, HEAD), F32),
        ),
        in_specs=[vmem] * 4,
        out_specs=(vmem, vmem),
        scratch_shapes=[
            pltpu.VMEM((rows, HEAD), BF16),
            pltpu.VMEM((rows, HEAD), BF16),
            pltpu.VMEM((HEAD, rows), BF16),
            pltpu.VMEM((rows, Q_ROWS), F32),
            pltpu.VMEM((rows, Q_ROWS), F32),
            pltpu.VMEM((rows, Q_ROWS), BF16),
            pltpu.VMEM((rows, HEAD), F32),
            pltpu.VMEM((rows, HEAD), F32),
            pltpu.VMEM((16, HEAD), F32),
        ],
        compiler_params=pltpu.CompilerParams(vmem_limit_bytes=48 * 1024 * 1024),
        cost_estimate=pl.CostEstimate(
            flops=10 * rows * rows * HEAD, bytes_accessed=8 * rows * HEAD, transcendentals=rows * rows
        ),
        name="attention",
    )(triple, upstream, query_gain.reshape(1, HEAD), key_gain.reshape(1, HEAD))


def local(image_input, text_input, w_qkv, query_gain, key_gain, image_cotangent, text_cotangent):
    own_index = lax.axis_index(SEQ)
    offset = own_index * HEAD
    features = image_input.shape[2]
    image_rows_dev = image_input.shape[1]
    text_rows = text_input.shape[1]
    own = lax.dynamic_slice_in_dim(w_qkv, offset, HEAD, 2).reshape(w_qkv.shape[0], 3 * HEAD)
    weights = lax.all_gather(own, FSDP, axis=0, tiled=True)
    whole_image = lax.all_gather(image_input[0], SEQ, axis=0, tiled=True)
    image_rows = whole_image.shape[0]
    arrived = lax.all_to_all(image_cotangent[0], SEQ, split_axis=1, concat_axis=0, tiled=True)
    text_up = lax.dynamic_slice_in_dim(text_cotangent[0], offset, HEAD, 1)
    upstream = jnp.concatenate([arrived, text_up], axis=0)
    tokens = jnp.concatenate([whole_image, text_input[0]], axis=0)
    triple = jnp.dot(tokens, weights, preferred_element_type=F32).astype(BF16)
    grads, gain_part = attention(triple, upstream, query_gain, key_gain)
    gain_total = lax.psum(gain_part, FSDP_SEQ)
    head_total = lax.dot_general(tokens, grads, (((0,), (0,)), ((), ())), preferred_element_type=F32)
    grad_weights = lax.psum_scatter(
        head_total.astype(BF16), FSDP, scatter_dimension=0, tiled=True
    ).astype(F32)
    partial = lax.dot_general(grads, weights, (((1,), (1,)), ((), ())), preferred_element_type=F32)
    partial = partial.astype(BF16)
    image_out = lax.psum_scatter(partial[:image_rows], SEQ, scatter_dimension=0, tiled=True)
    text_out = lax.psum(partial[image_rows:], SEQ)
    return (
        image_out.reshape(1, image_rows_dev, features),
        text_out.reshape(1, text_rows, features),
        grad_weights.reshape(-1, 3, HEAD),
        gain_total,
    )


def solution(mesh):
    finer = Mesh(
        mesh.devices.reshape(2, 4, 2, 4, 2), ("fsdp_0", "fsdp_1", "seq_0", "seq_1", "seq_2")
    )
    return jax.shard_map(
        local,
        mesh=finer,
        in_specs=(
            P(FSDP, SEQ, None),
            P(FSDP, None, None),
            P(FSDP, None, None),
            P(),
            P(),
            P(FSDP, SEQ, None),
            P(FSDP, None, None),
        ),
        out_specs=(P(FSDP, SEQ, None), P(FSDP, None, None), P(FSDP, None, SEQ), P()),
        check_vma=False,
    )
```

time: 571 us -> 434 us (0.76)
  matrix products: 124 us -> 17 us
  other arithmetic: 74.9 us -> 1.68 us
  waiting for transfers between devices: 237 us -> 289 us
  local copies, waits for them, and re-layouts: 58.3 us -> 17.5 us
  blocking collectives: 33.6 us -> 64.8 us
  Pallas kernels: 0 us -> 19.1 us
  starting transfers between devices: 24.2 us -> 9.66 us
    all_gather x2, waiting for transfers between devices: 195 us -> 82.9 us  [the longest x1 71.2 us: local(): whole_image = lax.all_gather(image_input[0], SEQ, axis=0, tiled=True)]
    dot_general x41 -> x3, matrix products: 124 us -> 17 us  [the longest x1 6.86 us: local(): triple = jnp.dot(tokens, weights, preferred_element_type=F32).astype(BF16)]
    psum x0 -> x1, waiting for transfers between devices: none -> 97.1 us  [local(): text_out = lax.psum(partial[image_rows:], SEQ)]
    reduce_scatter x1 -> x2, waiting for transfers between devices: 0.01 us -> 94.2 us  [the longest x1 94.2 us: local(): lax.psum_scatter(partial[:image_rows], SEQ, scatter_dimension=0, tiled=True)]
    add x16 -> x0, other arithmetic: 50.8 us -> none  [add_block(): return running + rounded.astype(jnp.float32)]
    psum x5 -> x1, blocking collectives: 33.6 us -> 64.8 us  [local(): gain_total = lax.psum(gain_part, FSDP_SEQ)]
    all_to_all x4 -> x1, waiting for transfers between devices: 41.6 us -> 14.3 us  [local(): lax.all_to_all(image_cotangent[0], SEQ, split_axis=1, concat_axis=0, tile...]
    pallas_call x0 -> x1, Pallas kernels: none -> 19.1 us  [attention(): pl.pallas_call(attention_kernel, out_shape=(jax.ShapeDtypeStruct((rows, 3...]
  transfers between devices with their start and end apart: 7 -> 6, of which waited for: 4 -> 5; matrix products, arithmetic and copies ran while one was open for 40% -> 4% of each run, Pallas kernels for 0% -> 0%
where the time goes in v1:
time: 434 us; the launch traced here: 433 us
  waiting for transfers between devices  289 us (67%)
  blocking collectives  64.8 us (15%)
  Pallas kernels  19.1 us (4%)
  local copies, waits for them, and re-layouts  17.5 us (4%)
  matrix products  17 us (4%)
  between operations  13.9 us (3%)
  starting transfers between devices  9.66 us (2%)
    psum x1, waiting for transfers between devices, local(): text_out = lax.psum(partial[image_rows:], SEQ)  97.1 us
    reduce_scatter x1, waiting for transfers between devices, local(): lax.psum_scatter(partial[:image_rows], SEQ, scatter_dimension=0, tiled=True)  94.2 us
    all_gather x1, waiting for transfers between devices, local(): whole_image = lax.all_gather(image_input[0], SEQ, axis=0, tiled=True)  71.2 us
    psum x1, blocking collectives, local(): gain_total = lax.psum(gain_part, FSDP_SEQ)  64.8 us
    pallas_call x1, Pallas kernels, attention(): pl.pallas_call(attention_kernel, out_shape=(jax.ShapeDtypeStruct((rows, 3...  19.1 us
    all_to_all x1, waiting for transfers between devices, local(): lax.all_to_all(image_cotangent[0], SEQ, split_axis=1, concat_axis=0, tile...  14.3 us
    all_gather x1, waiting for transfers between devices, local(): weights = lax.all_gather(own, FSDP, axis=0, tiled=True)  11.7 us
    all_to_all x1, starting transfers between devices, local(): lax.all_to_all(image_cotangent[0], SEQ, split_axis=1, concat_axis=0, tile...  9.28 us
  transfers between devices with their start and end apart: 6, of which 5 were waited for; matrix products, arithmetic and copies ran while one was open for 4% of the time, Pallas kernels for 0%

profile of v1, /device:TPU:1, one launch (start us, length us, event | category | flops | bytes accessed | tf_op | source)
XLA Modules:
  0.0 432.8 jit_solution(6483955572312483514)
XLA Ops:
  7.2 0.0 copy-start
  7.2 0.0 all-gather.4.cloned.1.call-start
  7.2 1.6 copy-done
  8.8 0.7 copy_bitcast_fusion.1
  9.5 0.0 all-gather.4.cloned.1.call-update
  9.6 0.0 all-gather.6.cloned.1.call-start
  9.6 0.7 all-gather.6.cloned.1.call-update
  10.3 1.1 copy.18
  11.5 0.9 copy.14
  12.4 9.3 %all-to-all-start = ((bf16[128,16,128]{2,0,1:T(8,128)(2,1)}), bf16[128,16,128]{2,0,1:T(8,128)(2,1)S(1)}, u32[]{:S(2)}, u32[]{:S(2)}) async-start(bf16[128,16,128]{2,0,1:T(8,128)(2,1)} %copy.14), calls=%async_computation | async-start | bytes 1048576 | tf_op jit(solution)/shard_map/all_to_all | solution.py:150
  21.7 0.0 reduce-scatter.5.cloned.1.call-start
  21.7 0.8 dynamic-slice_bitcast_fusion.1
  22.5 14.3 %all-to-all-done = bf16[128,16,128]{2,0,1:T(8,128)(2,1)S(1)} async-done(((bf16[128,16,128]{2,0,1:T(8,128)(2,1)}), bf16[128,16,128]{2,0,1:T(8,128)(2,1)S(1)}, u32[]{:S(2)}, u32[]{:S(2)}) %all-to-all-start) | async-done | bytes 524320 | tf_op jit(solution)/shard_map/all_to_all | solution.py:150
  36.9 11.7 %all-gather.4.cloned.1.call-done = bf16[1536,384]{1,0:T(8,128)(2,1)} async-done(((bf16[192,384]{1,0:T(8,128)(2,1)}), bf16[1536,384]{1,0:T(8,128)(2,1)}) %all-gather.4.cloned.1.call-update) | async-done | bytes 1179664 | tf_op jit(solution)/shard_map/all_gather | solution.py:147
  48.5 71.2 %all-gather.6.cloned.1.call-done = bf16[1,2048,1536]{2,1,0:T(8,128)(2,1)} async-done(((bf16[1,128,1536]{2,1,0:T(8,128)(2,1)}), bf16[1,2048,1536]{2,1,0:T(8,128)(2,1)}) %all-gather.6.cloned.1.call-update) | async-done | bytes 6291472 | tf_op jit(solution)/shard_map/all_gather | solution.py:148
  119.7 0.0 copy-start.1
  119.7 0.0 copy-start.2
  119.7 6.9 %fusion.2.triple = bf16[2176,384]{1,0:T(8,128)(2,1)S(1)} fusion(bf16[1536,384]{1,0:T(8,128)(2,1)} %all-gather.4.cloned.1.call-done, bf16[128,1536]{1,0:T(8,128)(2,1)} %bitcast.36, bf16[2048,1536]{1,0:T(8,128)(2,1)} %bitcast.34), kind=kOutput, calls=%fused_computation.4 | convolution fusion | flops 2581118976 | bytes 9535488 | tf_op jit(solution)/shard_map/dot_general | solution.py:154
  126.6 0.0 copy-done.1
  126.6 0.0 copy-done.2
  126.6 0.0 copy-start.5
  126.6 0.0 copy-start.7
  126.6 19.1 %attention.1 = (bf16[2176,384]{1,0:T(8,128)(2,1)S(1)}, f32[2,128]{1,0:T(2,128)S(1)}) custom-call(bf16[2176,384]{1,0:T(8,128)(2,1)S(1)} %fusion.2.triple, bf16[2176,128]{1,0:T(8,128)(2,1)S(1)} %pad_maximum_fusion.7.upstream, f32[1,128]{1,0:T(1,128)S(1)} %bitcast.29, f32[1,128]{1,0:T(1,128)S(1)} %bitcast.30), custom_call_target="tpu_custom_call" | custom-call | flops 6060769280 | bytes 2228224 | tf_op jit(solution)/shard_map/attention/pallas_call | solution.py:113
  145.8 0.0 copy-start.3
  145.8 1.2 copy-done.3
  146.9 0.0 copy-done.5
  146.9 0.0 copy-done.7
  146.9 0.0 copy-start.6
  147.0 4.8 %fusion.3 = bf16[1536,384]{1,0:T(8,128)(2,1)} fusion(bf16[2176,384]{1,0:T(8,128)(2,1)S(1)} %get-tuple-element.6, bf16[128,1536]{1,0:T(8,128)(2,1)S(1)} %bitcast.37, bf16[2048,1536]{1,0:T(8,128)(2,1)S(1)} %bitcast.35), kind=kOutput, calls=%fused_computation.5 | convolution fusion | flops 2580873216 | bytes 9535488 | tf_op jit(solution)/shard_map/dot_general | solution.py:157
  151.8 0.0 reduce-scatter.5.cloned.1.call-update
  151.8 0.2 all-reduce.2.cloned.1.call-start
  152.0 0.0 copy-done.6
  152.0 5.3 %convolution_convert_fusion = bf16[2176,1536]{1,0:T(8,128)(2,1)S(1)} fusion(bf16[2176,384]{1,0:T(8,128)(2,1)} %copy-done.3, bf16[1536,384]{1,0:T(8,128)(2,1)S(1)} %copy-done.6), kind=kOutput, calls=%fused_computation | convolution fusion | flops 2570256384 | bytes 9535488 | tf_op jit(solution)/shard_map/dot_general | solution.py:161
  157.4 0.0 copy-start.4
  157.4 2.7 copy-done.4
  160.1 0.8 slice_bitcast_fusion
  160.9 0.0 all-reduce.2.cloned.1.call-update
  160.9 0.0 reduce-scatter.3.cloned.1.call-start
  161.0 5.8 %slice.8 = bf16[2048,1536]{1,0:T(8,128)(2,1)} slice(bf16[2176,1536]{1,0:T(8,128)(2,1)} %copy-done.4), slice={[0:2048], [0:1536]} | slice | bytes 12582912 | tf_op jit(solution)/shard_map/slice | solution.py:163
  166.8 0.0 reduce-scatter.3.cloned.1.call-update
  166.8 64.8 %psum.15 = f32[2,128]{1,0:T(2,128)} all-reduce(f32[2,128]{1,0:T(2,128)S(1)} %get-tuple-element.7), channel_id=1, replica_groups=mesh['fsdp_0'=2,'fsdp_1'=4,'seq_0'=2,'seq_1'=4,'seq_2'=2] {'fsdp_0','fsd..., use_global_device_ids=true, to_apply=%region_3.0 | all-reduce | flops 256 | bytes 2048 | tf_op jit(solution)/shard_map/psum | solution.py:156
  231.6 0.0 reduce-scatter.5.cloned.1.call-done
  231.6 1.6 copy_bitcast_fusion
  233.2 97.1 %all-reduce.2.cloned.1.call-done = bf16[1,128,1536]{2,1,0:T(8,128)(2,1)} async-done(((bf16[1,128,1536]{2,1,0:T(8,128)(2,1)}), bf16[1,128,1536]{2,1,0:T(8,128)(2,1)}) %all-reduce.2.cloned.1.call-update) | async-done | bytes 393232 | tf_op jit(solution)/shard_map/psum | solution.py:164
  330.3 94.2 %reduce-scatter.3.cloned.1.call-done = bf16[128,1536]{1,0:T(8,128)(2,1)} async-done(((bf16[2048,1536]{1,0:T(8,128)(2,1)}), bf16[128,1536]{1,0:T(8,128)(2,1)}) %reduce-scatter.3.cloned.1.call-update) | async-done | bytes 393232 | tf_op jit(solution)/shard_map/reduce_scatter | solution.py:163
  424.5 1.8 copy.22
  (1 shorter events, 0.0 us)
Async XLA Ops:
  7.2 1.7 copy-start
  7.2 41.4 %all-gather.4.cloned.1.call-start = ((), (), s32[]{:S(2)}) async-start(), calls=%async_computation.3 | async-start | bytes 1327104 | tf_op jit(solution)/shard_map/all_gather | solution.py:147
  9.6 110.2 %all-gather.6.cloned.1.call-start = ((), (), s32[]{:S(2)}) async-start(), calls=%async_computation.7 | async-start | bytes 6684672 | tf_op jit(solution)/shard_map/all_gather | solution.py:148
  12.4 24.4 %all-to-all-start = ((bf16[128,16,128]{2,0,1:T(8,128)(2,1)}), bf16[128,16,128]{2,0,1:T(8,128)(2,1)S(1)}, u32[]{:S(2)}, u32[]{:S(2)}) async-start(bf16[128,16,128]{2,0,1:T(8,128)(2,1)} %copy.14), calls=%async_computation | async-start | bytes 1048576 | tf_op jit(solution)/shard_map/all_to_all | solution.py:150
  21.7 209.9 %reduce-scatter.5.cloned.1.call-start = ((), (), s32[]{:S(2)}) async-start(), calls=%async_computation.6 | async-start | bytes 1327104 | tf_op jit(solution)/shard_map/reduce_scatter | solution.py:158
  119.7 6.9 %copy-start.1 = (f32[128]{0:T(128)S(1)}, f32[128]{0:T(128)}, u32[]{:S(2)}) copy-start(f32[128]{0:T(128)} %param.10) | copy-start | bytes 1540
  119.7 6.9 %copy-start.2 = (f32[128]{0:T(128)S(1)}, f32[128]{0:T(128)}, u32[]{:S(2)}) copy-start(f32[128]{0:T(128)} %param.11) | copy-start | bytes 1540
  126.6 20.3 %copy-start.5 = (bf16[1,2048,1536]{2,1,0:T(8,128)(2,1)S(1)}, bf16[1,2048,1536]{2,1,0:T(8,128)(2,1)}, u32[]{:S(2)}) copy-start(bf16[1,2048,1536]{2,1,0:T(8,128)(2,1)} %all-gather.6.cloned.1.call-done) | copy-start | bytes 18874372
  126.6 20.3 %copy-start.7 = (bf16[1,128,1536]{2,1,0:T(8,128)(2,1)S(1)}, bf16[1,128,1536]{2,1,0:T(8,128)(2,1)}, u32[]{:S(2)}) copy-start(bf16[1,128,1536]{2,1,0:T(8,128)(2,1)} %param.8) | copy-start | bytes 1179652
  145.8 1.2 copy-start.3
  146.9 5.1 %copy-start.6 = (bf16[1536,384]{1,0:T(8,128)(2,1)S(1)}, bf16[1536,384]{1,0:T(8,128)(2,1)}, u32[]{:S(2)}) copy-start(bf16[1536,384]{1,0:T(8,128)(2,1)} %all-gather.4.cloned.1.call-done) | copy-start | bytes 3538948
  151.8 178.5 %all-reduce.2.cloned.1.call-start = ((), (), s32[]{:S(2)}) async-start(), calls=%async_computation.5 | async-start | bytes 786432 | tf_op jit(solution)/shard_map/psum | solution.py:164
  157.4 2.7 copy-start.4
  160.9 263.6 %reduce-scatter.3.cloned.1.call-start = ((), (), s32[]{:S(2)}) async-start(), calls=%async_computation.4 | async-start | bytes 6684672 | tf_op jit(solution)/shard_map/reduce_scatter | solution.py:163
Sparse Core Ops, SparseCore 0:
  10.2 38.2 all-gather.3
  51.0 68.6 all-gather.5
  151.9 32.3 reduce-scatter.4
  187.2 143.0 all-reduce.1
  334.9 89.5 reduce-scatter.2

commit v2 on v1

--- a/solution.py
+++ b/solution.py
@@ -137,6 +137,293 @@
     )(triple, upstream, query_gain.reshape(1, HEAD), key_gain.reshape(1, HEAD))
 
 
+MESH = pl.DeviceIdType.MESH
+
+
+class Copies:
+    def __init__(self, send, recv):
+        self.send, self.recv, self.made = send, recv, []
+
+    def make(self, src, dst, to):
+        i = len(self.made)
+        copy = pltpu.make_async_remote_copy(
+            src_ref=src,
+            dst_ref=dst,
+            send_sem=self.send.at[i],
+            recv_sem=self.recv.at[i],
+            device_id=to,
+            device_id_type=MESH,
+        )
+        self.made.append(copy)
+        return copy
+
+
+def where():
+    return (
+        lax.axis_index("fsdp_0"),
+        lax.axis_index("fsdp_1"),
+        lax.axis_index("seq_0"),
+        lax.axis_index("seq_1"),
+        lax.axis_index("seq_2"),
+    )
+
+
+SEQ_OFFSETS = [(a, b, c) for a in range(2) for b in range(4) for c in range(2) if a + b + c > 0]
+FSDP_OFFSETS = [(a, b) for a in range(2) for b in range(4) if a + b > 0]
+
+
+def seq_peer(offset):
+    _, _, xh, z, core = where()
+    return (xh + offset[0]) % 2, (z + offset[1]) % 4, (core + offset[2]) % 2
+
+
+def fsdp_peer(offset):
+    xl, y, _, _, _ = where()
+    return (xl + offset[0]) % 2, (y + offset[1]) % 4
+
+
+def seq_id(peer):
+    return {"seq_0": peer[0], "seq_1": peer[1], "seq_2": peer[2]}
+
+
+def fsdp_id(peer):
+    return {"fsdp_0": peer[0], "fsdp_1": peer[1]}
+
+
+class Ring:
+    def __init__(self, copies, slot, pair_axis, pair, ring_axis, ring):
+        self.planes = (pair, 1 - pair)
+        self.ring = ring
+        after, before = {ring_axis: (ring + 1) % 4}, {ring_axis: (ring + 3) % 4}
+        other = {pair_axis: 1 - pair}
+
+        def same(piece, to):
+            return copies.make(piece, piece, to)
+
+        self.cross = [same(slot(pair, ring, h), other) for h in range(2)]
+        self.up = [[same(slot(p, ring, h), after) for h in range(2)] for p in self.planes]
+        self.down = [[same(slot(p, ring, h), before) for h in range(2)] for p in self.planes]
+        self.pass_up = [same(slot(p, (ring + 3) % 4, 0), after) for p in self.planes]
+        self.pass_down = [same(slot(p, (ring + 1) % 4, 1), before) for p in self.planes]
+
+
+IMAGE_CHUNK = 128
+IMAGE_ROWS = 2048
+WEIGHT_ROWS = 192
+
+
+def gather_kernel(
+    image, text, own_weights, cotangent, text_cotangent,
+    tokens_out, weights_out, triple_out, upstream_out,
+    tokens, weights, triple, upstream, send, recv, local_sems,
+):
+    xl, y, xh, z, core = where()
+    own = (xh * 4 + z) * 2 + core
+    half = IMAGE_CHUNK // 2
+
+    def rows(p, r, c, h):
+        return pl.ds(pl.multiple_of(((p * 4 + r) * 2 + c) * IMAGE_CHUNK + h * half, half), half)
+
+    def token_slot(p, r, h):
+        return tokens.at[rows(p, r, core, h), :]
+
+    whalf = WEIGHT_ROWS // 2
+
+    def weight_slot(p, r, h):
+        return weights.at[
+            pl.ds(pl.multiple_of((p * 4 + r) * WEIGHT_ROWS + h * whalf, whalf), whalf), :
+        ]
+
+    barrier = pltpu.get_barrier_semaphore()
+    greeted = [seq_id(seq_peer(o)) for o in SEQ_OFFSETS] + [
+        fsdp_id(fsdp_peer(o)) for o in ((1, 0), (0, 1), (0, 3))
+    ]
+    for peer in greeted:
+        pl.semaphore_signal(barrier, inc=1, device_id=peer, device_id_type=MESH)
+
+    def columns(s):
+        return pl.ds(pl.multiple_of(s * HEAD, HEAD), HEAD)
+
+    def chunk(s):
+        return pl.ds(pl.multiple_of(s * IMAGE_CHUNK, IMAGE_CHUNK), IMAGE_CHUNK)
+
+    text_rows = pl.ds(IMAGE_ROWS, text.shape[0])
+    fills = [
+        pltpu.make_async_copy(image, tokens.at[chunk(own), :], local_sems.at[0]),
+        pltpu.make_async_copy(
+            own_weights,
+            weights.at[pl.ds(pl.multiple_of((xl * 4 + y) * WEIGHT_ROWS, WEIGHT_ROWS), WEIGHT_ROWS), :],
+            local_sems.at[1],
+        ),
+        pltpu.make_async_copy(text, tokens.at[text_rows, :], local_sems.at[2]),
+        pltpu.make_async_copy(
+            cotangent.at[:, columns(own)], upstream.at[chunk(own), :], local_sems.at[3]
+        ),
+        pltpu.make_async_copy(
+            text_cotangent.at[:, columns(own)], upstream.at[text_rows, :], local_sems.at[4]
+        ),
+    ]
+    for fill in fills:
+        fill.start()
+
+    copies = Copies(send, recv)
+    token_ring = Ring(copies, token_slot, "seq_0", xh, "seq_1", z)
+    weight_ring = Ring(copies, weight_slot, "fsdp_0", xl, "fsdp_1", y)
+    shared = {}
+    for plane in range(2):
+        for d in range(4):
+            for h in range(2):
+                piece = token_slot(token_ring.planes[plane], (z + d) % 4, h)
+                shared[plane, d, h] = copies.make(piece, piece, {"seq_2": 1 - core})
+    exchanged = []
+    for offset in SEQ_OFFSETS:
+        peer = seq_peer(offset)
+        s = (peer[0] * 4 + peer[1]) * 2 + peer[2]
+        exchanged.append(
+            copies.make(cotangent.at[:, columns(s)], upstream.at[chunk(own), :], seq_id(peer))
+        )
+
+    fills[0].wait()
+    fills[1].wait()
+    pl.semaphore_wait(barrier, len(greeted))
+
+    t, w = token_ring, weight_ring
+    for h in range(2):
+        t.cross[h].start()
+        t.up[0][h].start()
+        t.down[0][1 - h].start()
+    for h in range(2):
+        w.cross[h].start()
+        w.up[0][h].start()
+        w.down[0][1 - h].start()
+    for h in range(2):
+        shared[0, 0, h].start()
+
+    def pass_on(ring, plane, then):
+        ring.up[plane][0].wait_recv()
+        ring.pass_up[plane].start()
+        then(3, 0)
+        ring.down[plane][1].wait_recv()
+        ring.pass_down[plane].start()
+        then(1, 1)
+
+    def nothing(d, h):
+        pass
+
+    def share(plane):
+        def then(d, h):
+            shared[plane, d, h].start()
+
+        return then
+
+    pass_on(t, 0, share(0))
+    pass_on(w, 0, nothing)
+    for h in range(2):
+        w.cross[h].wait_recv()
+        w.up[1][h].start()
+        w.down[1][h].start()
+    for h in range(2):
+        t.cross[h].wait_recv()
+        t.up[1][h].start()
+        t.down[1][h].start()
+        shared[1, 0, h].start()
+    t.up[0][1].wait_recv()
+    shared[0, 3, 1].start()
+    t.down[0][0].wait_recv()
+    shared[0, 1, 0].start()
+    for copy in exchanged:
+        copy.start()
+    pass_on(w, 1, nothing)
+    t.pass_up[0].wait_recv()
+    shared[0, 2, 0].start()
+    t.pass_down[0].wait_recv()
+    shared[0, 2, 1].start()
+    for plane in range(2):
+        w.up[plane][1].wait_recv()
+        w.down[plane][0].wait_recv()
+        w.pass_up[plane].wait_recv()
+        w.pass_down[plane].wait_recv()
+    weights_copy = pltpu.make_async_copy(weights, weights_out, local_sems.at[1])
+    weights_copy.start()
+    fills[2].wait()
+
+    def project(start, count):
+        at = pl.ds(start, count)
+        triple[at, :] = dot_nn(tokens[at, :], weights[...]).astype(BF16)
+
+    def project_pair(plane, d):
+        for h in range(2):
+            shared[plane, d, h].wait_recv()
+        p = token_ring.planes[plane]
+        project(pl.multiple_of((p * 4 + (z + d) % 4) * 2 * IMAGE_CHUNK, 2 * IMAGE_CHUNK), 2 * IMAGE_CHUNK)
+
+    project(IMAGE_ROWS, text.shape[0])
+    pass_on(t, 1, share(1))
+    for d in range(4):
+        project_pair(0, d)
+    t.up[1][1].wait_recv()
+    shared[1, 3, 1].start()
+    t.down[1][0].wait_recv()
+    shared[1, 1, 0].start()
+    project_pair(1, 0)
+    t.pass_up[1].wait_recv()
+    shared[1, 2, 0].start()
+    t.pass_down[1].wait_recv()
+    shared[1, 2, 1].start()
+    project_pair(1, 1)
+    project_pair(1, 3)
+    project_pair(1, 2)
+    tokens_copy = pltpu.make_async_copy(tokens, tokens_out, local_sems.at[0])
+    tokens_copy.start()
+    triple_copy = pltpu.make_async_copy(triple, triple_out, local_sems.at[2])
+    triple_copy.start()
+    for copy in exchanged:
+        copy.wait_recv()
+    fills[3].wait()
+    fills[4].wait()
+    upstream_copy = pltpu.make_async_copy(upstream, upstream_out, local_sems.at[3])
+    upstream_copy.start()
+    for copy in copies.made:
+        copy.wait_send()
+    for copy in (tokens_copy, weights_copy, triple_copy, upstream_copy):
+        copy.wait()
+
+
+def gather(image, text, own_weights, cotangent, text_cotangent):
+    features = image.shape[1]
+    total = IMAGE_ROWS + text.shape[0]
+    depth = 8 * WEIGHT_ROWS
+    anywhere = pl.BlockSpec(memory_space=pl.ANY)
+    n_copies = 2 * 14 + 16 + len(SEQ_OFFSETS)
+    return pl.pallas_call(
+        gather_kernel,
+        out_shape=(
+            jax.ShapeDtypeStruct((total, features), BF16),
+            jax.ShapeDtypeStruct((depth, 3 * HEAD), BF16),
+            jax.ShapeDtypeStruct((total, 3 * HEAD), BF16),
+            jax.ShapeDtypeStruct((total, HEAD), BF16),
+        ),
+        in_specs=[anywhere] * 5,
+        out_specs=(anywhere,) * 4,
+        scratch_shapes=[
+            pltpu.VMEM((total, features), BF16),
+            pltpu.VMEM((depth, 3 * HEAD), BF16),
+            pltpu.VMEM((total, 3 * HEAD), BF16),
+            pltpu.VMEM((total, HEAD), BF16),
+            pltpu.SemaphoreType.DMA((n_copies,)),
+            pltpu.SemaphoreType.DMA((n_copies,)),
+            pltpu.SemaphoreType.DMA((5,)),
+        ],
+        compiler_params=pltpu.CompilerParams(
+            collective_id=0, has_side_effects=True, vmem_limit_bytes=48 * 1024 * 1024
+        ),
+        cost_estimate=pl.CostEstimate(
+            flops=2 * total * features * 3 * HEAD, bytes_accessed=16 * 2**20, transcendentals=0
+        ),
+        name="gather",
+    )(image, text, own_weights, cotangent, text_cotangent)
+
+
 def local(image_input, text_input, w_qkv, query_gain, key_gain, image_cotangent, text_cotangent):
     own_index = lax.axis_index(SEQ)
     offset = own_index * HEAD
@@ -144,14 +431,10 @@
     image_rows_dev = image_input.shape[1]
     text_rows = text_input.shape[1]
     own = lax.dynamic_slice_in_dim(w_qkv, offset, HEAD, 2).reshape(w_qkv.shape[0], 3 * HEAD)
-    weights = lax.all_gather(own, FSDP, axis=0, tiled=True)
-    whole_image = lax.all_gather(image_input[0], SEQ, axis=0, tiled=True)
-    image_rows = whole_image.shape[0]
-    arrived = lax.all_to_all(image_cotangent[0], SEQ, split_axis=1, concat_axis=0, tiled=True)
-    text_up = lax.dynamic_slice_in_dim(text_cotangent[0], offset, HEAD, 1)
-    upstream = jnp.concatenate([arrived, text_up], axis=0)
-    tokens = jnp.concatenate([whole_image, text_input[0]], axis=0)
-    triple = jnp.dot(tokens, weights, preferred_element_type=F32).astype(BF16)
+    image_rows = IMAGE_ROWS
+    tokens, weights, triple, upstream = gather(
+        image_input[0], text_input[0], own, image_cotangent[0], text_cotangent[0]
+    )
     grads, gain_part = attention(triple, upstream, query_gain, key_gain)
     gain_total = lax.psum(gain_part, FSDP_SEQ)
     head_total = lax.dot_general(tokens, grads, (((0,), (0,)), ((), ())), preferred_element_type=F32)

time: 434 us -> 250 us (0.58)
  waiting for transfers between devices: 289 us -> 72.7 us
  Pallas kernels: 19.1 us -> 64.5 us
  starting transfers between devices: 9.66 us -> 0.12 us
  matrix products: 17 us -> 10.2 us
    reduce_scatter x1, waiting for transfers between devices: 94.2 us -> 0.01 us  [local(): lax.psum_scatter(partial[:image_rows], SEQ, scatter_dimension=0, tiled=True)]
    all_gather x2 -> x0, waiting for transfers between devices: 82.9 us -> none  [the longest x1 71.2 us: local(): whole_image = lax.all_gather(image_input[0], SEQ, axis=0, tiled=True)]
    pallas_call x0 -> x1, Pallas kernels: none -> 45.6 us  [gather(): pl.pallas_call(gather_kernel, out_shape=(jax.ShapeDtypeStruct((total, fea...]
    psum x1, waiting for transfers between devices: 97.1 us -> 72.7 us  [local(): text_out = lax.psum(partial[image_rows:], SEQ)]
    all_to_all x1 -> x0, waiting for transfers between devices: 14.3 us -> none  [local(): lax.all_to_all(image_cotangent[0], SEQ, split_axis=1, concat_axis=0, tile...]
    all_to_all x1 -> x0, starting transfers between devices: 9.28 us -> none  [local(): lax.all_to_all(image_cotangent[0], SEQ, split_axis=1, concat_axis=0, tile...]
    dot_general x1 -> x0, matrix products: 6.86 us -> none  [local(): triple = jnp.dot(tokens, weights, preferred_element_type=F32).astype(BF16)]
    unnamed x18 -> x21, local copies, waits for them, and re-layouts: 8.45 us -> 11.4 us
  transfers between devices with their start and end apart: 6 -> 3, of which waited for: 5 -> 1; matrix products, arithmetic and copies ran while one was open for 4% -> 5% of each run, Pallas kernels for 0% -> 0%
where the time goes in v2:
time: 250 us; the launch traced here: 249 us
  waiting for transfers between devices  72.7 us (29%)
  blocking collectives  66.4 us (27%)
  Pallas kernels  64.5 us (26%)
  local copies, waits for them, and re-layouts  18 us (7%)
  between operations  15.6 us (6%)
  matrix products  10.2 us (4%)
    psum x1, waiting for transfers between devices, local(): text_out = lax.psum(partial[image_rows:], SEQ)  72.7 us
    psum x1, blocking collectives, local(): gain_total = lax.psum(gain_part, FSDP_SEQ)  66.4 us
    pallas_call x1, Pallas kernels, gather(): pl.pallas_call(gather_kernel, out_shape=(jax.ShapeDtypeStruct((total, fea...  45.6 us
    pallas_call x1, Pallas kernels, attention(): pl.pallas_call(attention_kernel, out_shape=(jax.ShapeDtypeStruct((rows, 3...  18.9 us
    unnamed x21, local copies, waits for them, and re-layouts  11.4 us
    slice x1, local copies, waits for them, and re-layouts, local(): partial[:image_rows]  5.82 us
    dot_general x1, matrix products, local(): lax.dot_general(grads, weights, (((1,), (1,)), ((), ())), preferred_eleme...  5.34 us
  transfers between devices with their start and end apart: 3, of which 1 were waited for; matrix products, arithmetic and copies ran while one was open for 5% of the time, Pallas kernels for 0%

profile of v2, /device:TPU:1, one launch (start us, length us, event | category | flops | bytes accessed | tf_op | source)
XLA Modules:
  0.0 249.1 jit_solution(6995861176940850617)
XLA Ops:
  8.0 0.0 copy-start
  8.0 0.0 reduce-scatter.5.cloned.1.call-start
  8.1 1.6 copy-done
  9.7 0.0 copy-start.1
  9.7 1.0 copy-done.1
  10.8 0.0 copy-start.2
  10.8 1.0 copy-done.2
  11.8 0.0 copy-start.3
  11.8 1.0 copy-done.3
  12.8 0.0 copy-start.4
  12.8 1.0 copy-done.4
  13.8 0.0 copy-start.5
  13.8 0.0 copy-start.6
  13.8 45.6 %gather.1 = (bf16[2176,1536]{1,0:T(8,128)(2,1)}, bf16[1536,384]{1,0:T(8,128)(2,1)S(1)}, bf16[2176,384]{1,0:T(8,128)(2,1)S(1)}, bf16[2176,128]{1,0:T(8,128)(2,1)S(1)}) custom-call(bf16[128,1536]{1,0:T(8,128)(2,1)S(1)} %bitcast.25, bf16[128,1536]{1,0:T(8,128)(2,1)S(1)} %bitcast.26, bf16[192,384]{1,0:T(8,128)(2,1)S(1)} %copy_bitcast_fusion.1.own_weights, ...), custom_call_target="tpu_custom_call" | custom-call | flops 2566914048 | bytes 16777216 | tf_op jit(solution)/shard_map/gather/pallas_call | solution.py:398
  59.4 0.0 copy-done.5
  59.4 0.0 copy-done.6
  59.4 0.0 copy-start.9
  59.4 18.9 %attention.1 = (bf16[2176,384]{1,0:T(8,128)(2,1)S(1)}, f32[2,128]{1,0:T(2,128)S(1)}) custom-call(bf16[2176,384]{1,0:T(8,128)(2,1)S(1)} %get-tuple-element.10.triple, bf16[2176,128]{1,0:T(8,128)(2,1)S(1)} %get-tuple-element.11.upstream, f32[1,128]{1,0:T(1,128)S(1)} %bitcast.27, f32[1,128]{1,0:T(1,128)S(1)} %bitcast.28), custom_call_target="tpu_custom_call" | custom-call | flops 6060769280 | bytes 2228224 | tf_op jit(solution)/shard_map/attention/pallas_call | solution.py:113
  78.3 0.0 copy-start.7
  78.3 1.2 copy-done.7
  79.5 0.0 copy-done.9
  79.5 4.8 %convolution_convert_fusion.1 = bf16[1536,384]{1,0:T(8,128)(2,1)} fusion(bf16[2176,1536]{1,0:T(8,128)(2,1)S(1)} %copy-done.9, bf16[2176,384]{1,0:T(8,128)(2,1)S(1)} %get-tuple-element.12), kind=kOutput, calls=%fused_computation.1 | convolution fusion | flops 2567503872 | bytes 9535488 | tf_op jit(solution)/shard_map/dot_general | solution.py:440
  84.3 0.0 reduce-scatter.5.cloned.1.call-update
  84.3 0.0 all-reduce.2.cloned.1.call-start
  84.4 5.3 %convolution_convert_fusion = bf16[2176,1536]{1,0:T(8,128)(2,1)S(1)} fusion(bf16[2176,384]{1,0:T(8,128)(2,1)} %copy-done.7, bf16[1536,384]{1,0:T(8,128)(2,1)S(1)} %get-tuple-element.13), kind=kOutput, calls=%fused_computation | convolution fusion | flops 2570256384 | bytes 9535488 | tf_op jit(solution)/shard_map/dot_general | solution.py:444
  89.7 0.0 copy-start.8
  89.7 2.7 %copy-done.8 = bf16[2176,1536]{1,0:T(8,128)(2,1)} copy-done((bf16[2176,1536]{1,0:T(8,128)(2,1)}, bf16[2176,1536]{1,0:T(8,128)(2,1)S(1)}, u32[]{:S(2)}) %copy-start.8) | copy-done | bytes 6684696
  92.5 0.8 slice_bitcast_fusion
  93.2 0.0 all-reduce.2.cloned.1.call-update
  93.3 0.0 reduce-scatter.3.cloned.1.call-start
  93.3 5.8 %slice.8 = bf16[2048,1536]{1,0:T(8,128)(2,1)} slice(bf16[2176,1536]{1,0:T(8,128)(2,1)} %copy-done.8), slice={[0:2048], [0:1536]} | slice | bytes 12582912 | tf_op jit(solution)/shard_map/slice | solution.py:446
  99.1 0.0 reduce-scatter.3.cloned.1.call-update
  99.2 66.4 %psum.15 = f32[2,128]{1,0:T(2,128)} all-reduce(f32[2,128]{1,0:T(2,128)S(1)} %get-tuple-element.15), channel_id=1, replica_groups=mesh['fsdp_0'=2,'fsdp_1'=4,'seq_0'=2,'seq_1'=4,'seq_2'=2] {'fsdp_0','fsd..., use_global_device_ids=true, to_apply=%region_3.0 | all-reduce | flops 256 | bytes 2048 | tf_op jit(solution)/shard_map/psum | solution.py:439
  165.6 0.0 reduce-scatter.5.cloned.1.call-done
  165.6 1.6 copy_bitcast_fusion
  167.3 72.7 %all-reduce.2.cloned.1.call-done = bf16[1,128,1536]{2,1,0:T(8,128)(2,1)} async-done(((bf16[1,128,1536]{2,1,0:T(8,128)(2,1)}), bf16[1,128,1536]{2,1,0:T(8,128)(2,1)}) %all-reduce.2.cloned.1.call-update) | async-done | bytes 393232 | tf_op jit(solution)/shard_map/psum | solution.py:447
  239.9 0.0 reduce-scatter.3.cloned.1.call-done
  239.9 1.8 copy.20
  (1 shorter events, 0.0 us)
Async XLA Ops:
  8.0 1.7 copy-start
  8.0 157.6 %reduce-scatter.5.cloned.1.call-start = ((), (), s32[]{:S(2)}) async-start(), calls=%async_computation.4 | async-start | bytes 1327104 | tf_op jit(solution)/shard_map/reduce_scatter | solution.py:441
  9.7 1.0 copy-start.1
  10.8 1.0 copy-start.2
  11.8 1.0 copy-start.3
  12.8 1.0 copy-start.4
  13.8 45.6 %copy-start.5 = (f32[128]{0:T(128)S(1)}, f32[128]{0:T(128)}, u32[]{:S(2)}) copy-start(f32[128]{0:T(128)} %param.10) | copy-start | bytes 1540
  13.8 45.6 %copy-start.6 = (f32[128]{0:T(128)S(1)}, f32[128]{0:T(128)}, u32[]{:S(2)}) copy-start(f32[128]{0:T(128)} %param.11) | copy-start | bytes 1540
  59.4 20.1 %copy-start.9 = (bf16[2176,1536]{1,0:T(8,128)(2,1)S(1)}, bf16[2176,1536]{1,0:T(8,128)(2,1)}, u32[]{:S(2)}) copy-start(bf16[2176,1536]{1,0:T(8,128)(2,1)} %get-tuple-element.14) | copy-start | bytes 20054020
  78.3 1.2 copy-start.7
  84.3 155.6 %all-reduce.2.cloned.1.call-start = ((), (), s32[]{:S(2)}) async-start(), calls=%async_computation.3 | async-start | bytes 786432 | tf_op jit(solution)/shard_map/psum | solution.py:447
  89.7 2.8 %copy-start.8 = (bf16[2176,1536]{1,0:T(8,128)(2,1)}, bf16[2176,1536]{1,0:T(8,128)(2,1)S(1)}, u32[]{:S(2)}) copy-start(bf16[2176,1536]{1,0:T(8,128)(2,1)S(1)} %convolution_convert_fusion) | copy-start | bytes 20054020
  93.3 146.7 %reduce-scatter.3.cloned.1.call-start = ((), (), s32[]{:S(2)}) async-start(), calls=%async_computation.2 | async-start | bytes 6684672 | tf_op jit(solution)/shard_map/reduce_scatter | solution.py:446
Sparse Core Ops, SparseCore 0:
  84.4 34.5 reduce-scatter.4
  123.8 92.4 reduce-scatter.2
Sparse Core Ops, SparseCore 1:
  93.4 146.5 all-reduce.1

commit v3 on v2

--- a/solution.py
+++ b/solution.py
@@ -424,6 +424,250 @@
     )(image, text, own_weights, cotangent, text_cotangent)
 
 
+def dot_tn(a, b):
+    return lax.dot_general(a, b, (((0,), (0,)), ((), ())), preferred_element_type=F32)
+
+
+PAIR_OFFSETS = [(a, b) for a in range(2) for b in range(4) if a + b > 0]
+
+
+def reduce_kernel(
+    tokens_in, weights_in, grads_in, gains_in,
+    image_out, text_out, weight_out, gain_out,
+    tokens, weights, grads, grads_other, sums, piece_out, piece_in, cross_out, cross_in,
+    dw_out, dw_in, text_part, text_in, text_all, gain_seq, gain_fsdp, send, recv, local_sems,
+):
+    xl, y, xh, z, core = where()
+    own = (xh * 4 + z) * 2 + core
+    group = xl * 4 + y
+    half = IMAGE_CHUNK // 2
+    planes = (xh, 1 - xh)
+    other_core = {"seq_2": 1 - core}
+
+    barrier = pltpu.get_barrier_semaphore()
+    greeted = [seq_id(seq_peer(o)) for o in SEQ_OFFSETS] + [
+        fsdp_id(fsdp_peer(o)) for o in FSDP_OFFSETS
+    ]
+    for peer in greeted:
+        pl.semaphore_signal(barrier, inc=1, device_id=peer, device_id_type=MESH)
+    fills = [
+        pltpu.make_async_copy(grads_in, grads, local_sems.at[0]),
+        pltpu.make_async_copy(weights_in, weights.at[0], local_sems.at[1]),
+        pltpu.make_async_copy(tokens_in, tokens, local_sems.at[2]),
+    ]
+    for fill in fills:
+        fill.start()
+
+    copies = Copies(send, recv)
+    to_other = [copies.make(weights.at[0], weights.at[1], other_core)]
+    for plane in (1, 0):
+        for d in (2, 1, 3, 0):
+            at = planes[plane] * 4 + (z + d) % 4
+            to_other.append(
+                copies.make(
+                    grads.at[pl.ds(pl.multiple_of((at * 2 + 1 - core) * IMAGE_CHUNK, IMAGE_CHUNK), IMAGE_CHUNK), :],
+                    grads_other.at[pl.ds(pl.multiple_of(at * IMAGE_CHUNK, IMAGE_CHUNK), IMAGE_CHUNK), :],
+                    other_core,
+                )
+            )
+    text_half = text_out.shape[0] // 2
+    text_mine = pl.ds(pl.multiple_of(IMAGE_ROWS + core * text_half, text_half), text_half)
+    text_theirs = pl.ds(pl.multiple_of(IMAGE_ROWS + (1 - core) * text_half, text_half), text_half)
+    text_got = pl.ds(IMAGE_ROWS // 2, text_half)
+    to_other.append(copies.make(grads.at[text_theirs, :], grads_other.at[text_got, :], other_core))
+
+    gain_first = [
+        copies.make(gain_seq.at[own], gain_seq.at[own], seq_id(seq_peer(o))) for o in SEQ_OFFSETS
+    ]
+    gain_second = [
+        copies.make(gain_fsdp.at[group], gain_fsdp.at[group], fsdp_id(fsdp_peer(o)))
+        for o in FSDP_OFFSETS
+    ]
+    dw_sends = []
+    for o in FSDP_OFFSETS:
+        peer = fsdp_peer(o)
+        dw_sends.append(copies.make(dw_out.at[peer[0] * 4 + peer[1]], dw_in.at[group], fsdp_id(peer)))
+    text_first, text_second = [], []
+    for o in PAIR_OFFSETS:
+        peer = seq_peer((o[0], o[1], 0))
+        to = {"seq_0": peer[0], "seq_1": peer[1]}
+        text_first.append(copies.make(text_part.at[peer[0], peer[1]], text_in.at[xh, z], to))
+        text_second.append(copies.make(text_all.at[core, xh, z], text_all.at[core, xh, z], to))
+    text_third = copies.make(text_all.at[core], text_all.at[core], other_core)
+    up, down = {"seq_1": (z + 1) % 4}, {"seq_1": (z + 3) % 4}
+    pieces = {}
+    for plane in range(2):
+        for i in range(6):
+            pieces[plane, i] = copies.make(
+                piece_out.at[plane, i], piece_in.at[plane, i], up if i < 3 else down
+            )
+    cross = [copies.make(cross_out.at[h], cross_in.at[h], {"seq_0": 1 - xh}) for h in range(2)]
+
+    gain_seq[own] = jnp.zeros(gain_seq.shape[1:], F32)
+    gain_seq[own, 0:2, :] = gains_in[...]
+    fills[0].wait()
+    fills[1].wait()
+    pl.semaphore_wait(barrier, len(greeted))
+    for copy in to_other + gain_first:
+        copy.start()
+    fills[2].wait()
+
+    def weight_part(j):
+        block = 2 * WEIGHT_ROWS
+        part = dot_tn(tokens[:, j * block : (j + 1) * block], grads[...]).astype(BF16)
+        dw_out[2 * j] = part[:WEIGHT_ROWS]
+        dw_out[2 * j + 1] = part[WEIGHT_ROWS:]
+
+    def input_part(mine, theirs):
+        return dot_nt(grads[mine, :], weights[0]) + dot_nt(grads_other[theirs, :], weights[1])
+
+    def add_up(plane, d):
+        at = planes[plane] * 4 + (z + d) % 4
+        mine = pl.ds(pl.multiple_of((at * 2 + core) * IMAGE_CHUNK, IMAGE_CHUNK), IMAGE_CHUNK)
+        theirs = pl.ds(pl.multiple_of(at * IMAGE_CHUNK, IMAGE_CHUNK), IMAGE_CHUNK)
+        sums[plane, d] = input_part(mine, theirs)
+
+    halves = (pl.ds(0, half), pl.ds(half, half))
+
+    def put(plane, i, value):
+        piece_out[plane, i] = value.astype(BF16)
+        pieces[plane, i].start()
+
+    def arrived(plane, i):
+        return piece_in[plane, i].astype(F32)
+
+    weight_part(0)
+    weight_part(1)
+    for copy in to_other:
+        copy.wait_recv()
+
+    def first_sends(plane):
+        add_up(plane, 2)
+        put(plane, 0, sums[plane, 2, halves[0], :])
+        put(plane, 3, sums[plane, 2, halves[1], :])
+        add_up(plane, 1)
+        put(plane, 1, sums[plane, 1, halves[1], :])
+        add_up(plane, 3)
+        put(plane, 4, sums[plane, 3, halves[0], :])
+
+    def pass_on(plane):
+        pieces[plane, 0].wait_recv()
+        put(plane, 2, sums[plane, 1, halves[0], :] + arrived(plane, 0))
+        pieces[plane, 3].wait_recv()
+        put(plane, 5, sums[plane, 3, halves[1], :] + arrived(plane, 3))
+
+    def finish(plane, h):
+        first, second = (2, 4) if h == 0 else (1, 5)
+        pieces[plane, first].wait_recv()
+        pieces[plane, second].wait_recv()
+        return sums[plane, 0, halves[h], :] + arrived(plane, first) + arrived(plane, second)
+
+    first_sends(1)
+    text_sum = input_part(text_mine, text_got).astype(BF16)
+    rows, columns = text_part.shape[2:]
+    for a in range(2):
+        for b in range(4):
+            text_part[a, b] = text_sum[b * rows : (b + 1) * rows, a * columns : (a + 1) * columns]
+    for copy in text_first:
+        copy.start()
+    text_in[xh, z] = text_part[xh, z]
+    weight_part(2)
+    pass_on(1)
+    weight_part(3)
+    for copy in dw_sends:
+        copy.start()
+    dw_in[group] = dw_out[group]
+    first_sends(0)
+    add_up(1, 0)
+    for copy in gain_first:
+        copy.wait_recv()
+    gain_fsdp[group] = jnp.sum(gain_seq[...], axis=0)
+    for copy in gain_second:
+        copy.start()
+    for copy in text_first:
+        copy.wait_recv()
+    text_all[core, xh, z] = jnp.sum(text_in[...].astype(F32), axis=(0, 1)).astype(BF16)
+    for copy in text_second:
+        copy.start()
+    for h in (1, 0):
+        cross_out[h] = finish(1, h).astype(BF16)
+        cross[h].start()
+    pass_on(0)
+    add_up(0, 0)
+    for copy in text_second:
+        copy.wait_recv()
+    text_third.start()
+    for copy in gain_second:
+        copy.wait_recv()
+    gain_out[...] = jnp.sum(gain_fsdp[...], axis=0)[0:2]
+    for copy in dw_sends:
+        copy.wait_recv()
+    weight_out[...] = jnp.sum(dw_in[...].astype(F32), axis=0)
+    text_third.wait_recv()
+    for c in range(2):
+        for a in range(2):
+            for b in range(4):
+                text_out[
+                    c * text_half + b * rows : c * text_half + (b + 1) * rows,
+                    a * columns : (a + 1) * columns,
+                ] = text_all[c, a, b]
+    for h in (1, 0):
+        total = finish(0, h)
+        cross[h].wait_recv()
+        image_out[halves[h], :] = (total + cross_in[h].astype(F32)).astype(BF16)
+    for copy in copies.made:
+        copy.wait_send()
+
+
+def reduce(tokens, weights, grads, gains):
+    total, features = tokens.shape
+    text_rows = total - IMAGE_ROWS
+    anywhere = pl.BlockSpec(memory_space=pl.ANY)
+    vmem = pl.BlockSpec(memory_space=pltpu.VMEM)
+    half = IMAGE_CHUNK // 2
+    n_copies = 10 + len(SEQ_OFFSETS) + 2 * len(FSDP_OFFSETS) + 2 * len(PAIR_OFFSETS) + 1 + 12 + 2
+    text_piece = (2, 4, text_rows // 8, features // 2)
+    return pl.pallas_call(
+        reduce_kernel,
+        out_shape=(
+            jax.ShapeDtypeStruct((IMAGE_CHUNK, features), BF16),
+            jax.ShapeDtypeStruct((text_rows, features), BF16),
+            jax.ShapeDtypeStruct((WEIGHT_ROWS, 3 * HEAD), F32),
+            jax.ShapeDtypeStruct((2, HEAD), F32),
+        ),
+        in_specs=[anywhere, anywhere, anywhere, vmem],
+        out_specs=(vmem,) * 4,
+        scratch_shapes=[
+            pltpu.VMEM((total, features), BF16),
+            pltpu.VMEM((2, features, 3 * HEAD), BF16),
+            pltpu.VMEM((total, 3 * HEAD), BF16),
+            pltpu.VMEM((total // 2, 3 * HEAD), BF16),
+            pltpu.VMEM((2, 4, IMAGE_CHUNK, features), F32),
+            pltpu.VMEM((2, 6, half, features), BF16),
+            pltpu.VMEM((2, 6, half, features), BF16),
+            pltpu.VMEM((2, half, features), BF16),
+            pltpu.VMEM((2, half, features), BF16),
+            pltpu.VMEM((8, WEIGHT_ROWS, 3 * HEAD), BF16),
+            pltpu.VMEM((8, WEIGHT_ROWS, 3 * HEAD), BF16),
+            pltpu.VMEM(text_piece, BF16),
+            pltpu.VMEM(text_piece, BF16),
+            pltpu.VMEM((2, *text_piece), BF16),
+            pltpu.VMEM((16, 8, HEAD), F32),
+            pltpu.VMEM((8, 8, HEAD), F32),
+            pltpu.SemaphoreType.DMA((n_copies,)),
+            pltpu.SemaphoreType.DMA((n_copies,)),
+            pltpu.SemaphoreType.DMA((3,)),
+        ],
+        compiler_params=pltpu.CompilerParams(
+            collective_id=1, has_side_effects=True, vmem_limit_bytes=56 * 1024 * 1024
+        ),
+        cost_estimate=pl.CostEstimate(
+            flops=4 * total * features * 3 * HEAD, bytes_accessed=16 * 2**20, transcendentals=0
+        ),
+        name="reduce",
+    )(tokens, weights, grads, gains)
+
+
 def local(image_input, text_input, w_qkv, query_gain, key_gain, image_cotangent, text_cotangent):
     own_index = lax.axis_index(SEQ)
     offset = own_index * HEAD
@@ -431,20 +675,11 @@
     image_rows_dev = image_input.shape[1]
     text_rows = text_input.shape[1]
     own = lax.dynamic_slice_in_dim(w_qkv, offset, HEAD, 2).reshape(w_qkv.shape[0], 3 * HEAD)
-    image_rows = IMAGE_ROWS
     tokens, weights, triple, upstream = gather(
         image_input[0], text_input[0], own, image_cotangent[0], text_cotangent[0]
     )
     grads, gain_part = attention(triple, upstream, query_gain, key_gain)
-    gain_total = lax.psum(gain_part, FSDP_SEQ)
-    head_total = lax.dot_general(tokens, grads, (((0,), (0,)), ((), ())), preferred_element_type=F32)
-    grad_weights = lax.psum_scatter(
-        head_total.astype(BF16), FSDP, scatter_dimension=0, tiled=True
-    ).astype(F32)
-    partial = lax.dot_general(grads, weights, (((1,), (1,)), ((), ())), preferred_element_type=F32)
-    partial = partial.astype(BF16)
-    image_out = lax.psum_scatter(partial[:image_rows], SEQ, scatter_dimension=0, tiled=True)
-    text_out = lax.psum(partial[image_rows:], SEQ)
+    image_out, text_out, grad_weights, gain_total = reduce(tokens, weights, grads, gain_part)
     return (
         image_out.reshape(1, image_rows_dev, features),
         text_out.reshape(1, text_rows, features),

time: 250 us -> 126 us (0.50)
  waiting for transfers between devices: 72.7 us -> 0 us
  blocking collectives: 66.4 us -> 0 us
  Pallas kernels: 64.5 us -> 110 us
  between operations: 15.6 us -> 0.7 us
  matrix products: 10.2 us -> 0 us
  local copies, waits for them, and re-layouts: 18 us -> 15 us
    psum x1 -> x0, waiting for transfers between devices: 72.7 us -> none  [local(): text_out = lax.psum(partial[image_rows:], SEQ)]
    psum x1 -> x0, blocking collectives: 66.4 us -> none  [local(): gain_total = lax.psum(gain_part, FSDP_SEQ)]
    pallas_call x0 -> x1, Pallas kernels: none -> 45.3 us  [reduce(): pl.pallas_call(reduce_kernel, out_shape=(jax.ShapeDtypeStruct((IMAGE_CHUN...]
    dot_general x2 -> x0, matrix products: 10.2 us -> none  [the longest x1 5.34 us: local(): lax.dot_general(grads, weights, (((1,), (1,)), ((), ())), preferred_eleme...]
    slice x1 -> x0, local copies, waits for them, and re-layouts: 5.82 us -> none  [local(): partial[:image_rows]]
    unnamed x21 -> x24, local copies, waits for them, and re-layouts: 11.4 us -> 15 us
  transfers between devices with their start and end apart: 3 -> 0, of which waited for: 1 -> 0; matrix products, arithmetic and copies ran while one was open for 5% -> 0% of each run, Pallas kernels for 0% -> 0%
where the time goes in v3:
time: 126 us
  Pallas kernels  110 us (87%)
  local copies, waits for them, and re-layouts  15 us (12%)
    pallas_call x1, Pallas kernels, gather(): pl.pallas_call(gather_kernel, out_shape=(jax.ShapeDtypeStruct((total, fea...  45.6 us
    pallas_call x1, Pallas kernels, reduce(): pl.pallas_call(reduce_kernel, out_shape=(jax.ShapeDtypeStruct((IMAGE_CHUN...  45.3 us
    pallas_call x1, Pallas kernels, attention(): pl.pallas_call(attention_kernel, out_shape=(jax.ShapeDtypeStruct((rows, 3...  19 us
    unnamed x24, local copies, waits for them, and re-layouts  15 us

profile of v3, /device:TPU:1, one launch (start us, length us, event | category | flops | bytes accessed | tf_op | source)
XLA Modules:
  0.0 125.5 jit_solution(2095197204566332302)
XLA Ops:
  0.6 0.0 copy-start
  0.7 1.6 %copy-done = bf16[192,3,2048]{2,0,1:T(8,128)(2,1)S(1)} copy-done((bf16[192,3,2048]{2,0,1:T(8,128)(2,1)S(1)}, bf16[192,3,2048]{2,0,1:T(8,128)(2,1)}, u32[]{:S(2)}) %copy-start) | copy-done | bytes 2359320
  2.3 0.0 copy-start.1
  2.4 1.0 copy-done.1
  3.4 0.0 copy-start.2
  3.4 1.0 copy-done.2
  4.4 0.0 copy-start.3
  4.4 1.0 copy-done.3
  5.4 0.0 copy-start.4
  5.4 1.0 copy-done.4
  6.4 0.0 copy-start.5
  6.4 0.0 copy-start.6
  6.4 45.6 %gather.1 = (bf16[2176,1536]{1,0:T(8,128)(2,1)}, bf16[1536,384]{1,0:T(8,128)(2,1)S(1)}, bf16[2176,384]{1,0:T(8,128)(2,1)S(1)}, bf16[2176,128]{1,0:T(8,128)(2,1)S(1)}) custom-call(bf16[128,1536]{1,0:T(8,128)(2,1)S(1)} %bitcast.20, bf16[128,1536]{1,0:T(8,128)(2,1)S(1)} %bitcast.21, bf16[192,384]{1,0:T(8,128)(2,1)S(1)} %copy_bitcast_fusion.1.own_weights, ...), custom_call_target="tpu_custom_call" | custom-call | flops 2566914048 | bytes 16777216 | tf_op jit(solution)/shard_map/gather/pallas_call | solution.py:398
  52.0 0.0 copy-start.7
  52.0 1.1 copy-done.7
  53.1 0.0 copy-done.5
  53.1 0.0 copy-done.6
  53.1 19.0 %attention.1 = (bf16[2176,384]{1,0:T(8,128)(2,1)S(1)}, f32[2,128]{1,0:T(2,128)S(1)}) custom-call(bf16[2176,384]{1,0:T(8,128)(2,1)S(1)} %get-tuple-element.16.triple, bf16[2176,128]{1,0:T(8,128)(2,1)S(1)} %get-tuple-element.17.upstream, f32[1,128]{1,0:T(1,128)S(1)} %bitcast.22, f32[1,128]{1,0:T(1,128)S(1)} %bitcast.23), custom_call_target="tpu_custom_call" | custom-call | flops 6060769280 | bytes 2228224 | tf_op jit(solution)/shard_map/attention/pallas_call | solution.py:113
  72.1 0.0 copy-start.8
  72.1 1.2 copy-done.8
  73.3 0.0 copy-start.9
  73.3 0.6 copy-done.9
  73.9 45.3 %reduce.1 = (bf16[128,1536]{1,0:T(8,128)(2,1)}, bf16[128,1536]{1,0:T(8,128)(2,1)}, f32[192,384]{1,0:T(8,128)}, f32[2,128]{1,0:T(2,128)}) custom-call(bf16[2176,1536]{1,0:T(8,128)(2,1)} %get-tuple-element.14.tokens_in, bf16[1536,384]{1,0:T(8,128)(2,1)} %copy-done.7, bf16[2176,384]{1,0:T(8,128)(2,1)} %copy-done.8, f32[2,128]{1,0:T(2,128)} %copy-done.9), custom_call_target="tpu_custom_call" | custom-call | flops 5133828096 | bytes 16777216 | tf_op jit(solution)/shard_map/reduce/pallas_call | solution.py:630
  119.1 1.7 %copy_bitcast_fusion = f32[192,3,128]{2,0,1:T(8,128)} fusion(f32[192,384]{1,0:T(8,128)} %get-tuple-element.22), kind=kLoop, calls=%fused_computation | loop fusion | bytes 589824
  120.8 1.8 %copy.22 = bf16[1,128,1536]{2,1,0:T(8,128)(2,1)} copy(bf16[1,128,1536]{2,1,0:T(8,128)(2,1)} %bitcast.25) | data formatting | bytes 786432
  122.6 1.8 %copy.23 = bf16[1,128,1536]{2,1,0:T(8,128)(2,1)} copy(bf16[1,128,1536]{2,1,0:T(8,128)(2,1)} %bitcast.24) | data formatting | bytes 786432
  124.4 1.2 copy.24
  (1 shorter events, 0.0 us)
Async XLA Ops:
  0.6 1.7 %copy-start = (bf16[192,3,2048]{2,0,1:T(8,128)(2,1)S(1)}, bf16[192,3,2048]{2,0,1:T(8,128)(2,1)}, u32[]{:S(2)}) copy-start(bf16[192,3,2048]{2,0,1:T(8,128)(2,1)} %param.9) | copy-start | bytes 7077892
  2.3 1.0 copy-start.1
  3.4 1.0 copy-start.2
  4.4 1.0 copy-start.3
  5.4 1.0 copy-start.4
  6.4 46.7 %copy-start.5 = (f32[128]{0:T(128)S(1)}, f32[128]{0:T(128)}, u32[]{:S(2)}) copy-start(f32[128]{0:T(128)} %param.10) | copy-start | bytes 1540
  6.4 46.7 %copy-start.6 = (f32[128]{0:T(128)S(1)}, f32[128]{0:T(128)}, u32[]{:S(2)}) copy-start(f32[128]{0:T(128)} %param.11) | copy-start | bytes 1540
  52.0 1.1 copy-start.7
  72.1 1.2 copy-start.8
  73.3 0.6 copy-start.9

commit v4 on v1

v4 whole, which is shorter than its diff:
```python
import math

import jax
import jax.numpy as jnp
from jax import lax
from jax.experimental import pallas as pl
from jax.experimental.pallas import tpu as pltpu
from jax.sharding import Mesh
from jax.sharding import PartitionSpec as P

HEAD = 128
SEQ = ("seq_0", "seq_1", "seq_2")
FSDP = ("fsdp_0", "fsdp_1")
EPS = 1e-06
F32 = jnp.float32
BF16 = jnp.bfloat16
MESH = pl.DeviceIdType.MESH

Q_ROWS = 256
KEY_ROWS = 136
IMAGE_CHUNK = 128
IMAGE_ROWS = 2048
WEIGHT_ROWS = 192
WIDTH = 3 * HEAD


def dot_nt(a, b):
    return lax.dot_general(a, b, (((1,), (1,)), ((), ())), preferred_element_type=F32)


def dot_nn(a, b):
    return lax.dot_general(a, b, (((1,), (0,)), ((), ())), preferred_element_type=F32)


def dot_tn(a, b):
    return lax.dot_general(a, b, (((0,), (0,)), ((), ())), preferred_element_type=F32)


def folded(values):
    rows, width = values.shape
    return jnp.sum(values.reshape(rows // 8, 8, width), axis=0)


class Copies:
    def __init__(self, send, recv):
        self.send, self.recv, self.made = send, recv, []

    def make(self, src, dst, to):
        i = len(self.made)
        copy = pltpu.make_async_remote_copy(
            src_ref=src,
            dst_ref=dst,
            send_sem=self.send.at[i],
            recv_sem=self.recv.at[i],
            device_id=to,
            device_id_type=MESH,
        )
        self.made.append(copy)
        return copy


def where():
    return (
        lax.axis_index("fsdp_0"),
        lax.axis_index("fsdp_1"),
        lax.axis_index("seq_0"),
        lax.axis_index("seq_1"),
        lax.axis_index("seq_2"),
    )


SEQ_OFFSETS = [(a, b, c) for a in range(2) for b in range(4) for c in range(2) if a + b + c > 0]
FSDP_OFFSETS = [(a, b) for a in range(2) for b in range(4) if a + b > 0]
UNITS = [(a, b) for a in range(2) for b in range(4)]


def seq_peer(offset):
    _, _, xh, z, core = where()
    return (xh + offset[0]) % 2, (z + offset[1]) % 4, (core + offset[2]) % 2


def fsdp_peer(offset):
    xl, y, _, _, _ = where()
    return (xl + offset[0]) % 2, (y + offset[1]) % 4


def seq_id(peer):
    return {"seq_0": peer[0], "seq_1": peer[1], "seq_2": peer[2]}


def fsdp_id(peer):
    return {"fsdp_0": peer[0], "fsdp_1": peer[1]}


class GatherRing:
    def __init__(self, copies, slot, pair_axis, pair, ring_axis, ring):
        self.planes = (pair, 1 - pair)
        after, before = {ring_axis: (ring + 1) % 4}, {ring_axis: (ring + 3) % 4}
        other = {pair_axis: 1 - pair}

        def same(piece, to):
            return copies.make(piece, piece, to)

        self.cross = [same(slot(pair, ring, h), other) for h in range(2)]
        self.up = [[same(slot(p, ring, h), after) for h in range(2)] for p in self.planes]
        self.down = [[same(slot(p, ring, h), before) for h in range(2)] for p in self.planes]
        self.pass_up = same(slot(pair, (ring + 3) % 4, 0), after)
        self.pass_down = same(slot(pair, (ring + 1) % 4, 1), before)
        self.far = [same(slot(pair, (ring + 2) % 4, h), other) for h in range(2)]


GATHER_COPIES = 14


class ReduceRing:
    def __init__(self, copies, out, arrived, value, pair_axis, pair, ring_axis, ring):
        up, down = {ring_axis: (ring + 1) % 4}, {ring_axis: (ring + 3) % 4}
        other = {pair_axis: 1 - pair}
        to = [other] * 2 + [up] * 2 + [down] * 2 + [up] * 3 + [down] * 3 + [other] * 2
        self.out, self.arrived, self.value = out, arrived, value
        self.pieces = [copies.make(out.at[i], arrived.at[i], t) for i, t in enumerate(to)]

    def put(self, i, value):
        self.out[i] = value.astype(BF16)
        self.pieces[i].start()

    def got(self, i):
        self.pieces[i].wait_recv()
        return self.arrived[i].astype(F32)

    def send_far(self):
        self.put(0, self.value(1, 2, 0))
        self.put(1, self.value(1, 2, 1))

    def send_up(self):
        self.put(2, self.value(1, 1, 0))
        self.put(3, self.value(1, 1, 1))

    def send_down(self):
        self.put(4, self.value(1, 3, 0))
        self.put(5, self.value(1, 3, 1))

    def own_up(self):
        self.put(7, self.value(0, 1, 1))

    def own_down(self):
        self.put(10, self.value(0, 3, 0))

    def own_far(self):
        self.put(6, self.value(0, 2, 0) + self.got(0))
        self.put(9, self.value(0, 2, 1) + self.got(1))

    def pass_on(self):
        self.put(8, self.value(0, 1, 0) + self.got(6))
        self.put(11, self.value(0, 3, 1) + self.got(9))

    def cross(self):
        self.put(12, self.value(1, 0, 0) + self.got(2) + self.got(4))
        self.put(13, self.value(1, 0, 1) + self.got(3) + self.got(5))

    def total(self, h):
        parts = ((8, 10, 12), (7, 11, 13))[h]
        result = self.value(0, 0, h)
        for i in parts:
            result = result + self.got(i)
        return result


REDUCE_COPIES = 14


def step_kernel(
    image, text, w_qkv, qgain, kgain, cotangent, text_cotangent,
    image_out, text_out, weight_out, gain_out,
    tokens, weights, triple, upstream, qn, kn, kn_t, expd, esum, dsd, dpd, dv, gsum,
    grads, grads_other, dw, dx_out, dx_in, dw_out, dw_in,
    text_part, text_in, text_all, gain_seq, gain_fsdp, send, recv, local_sems,
):
    xl, y, xh, z, core = where()
    own = (xh * 4 + z) * 2 + core
    group = xl * 4 + y
    half = IMAGE_CHUNK // 2
    whalf = WEIGHT_ROWS // 2
    total_rows = tokens.shape[0]
    text_count = text.shape[0]
    text_rows = pl.ds(IMAGE_ROWS, text_count)
    factor = 1.0 / math.sqrt(HEAD)
    scale = factor * math.log2(math.e)
    planes = (xh, 1 - xh)
    other_core = {"seq_2": 1 - core}

    barrier = pltpu.get_barrier_semaphore()
    greeted = [seq_id(seq_peer(o)) for o in SEQ_OFFSETS] + [
        fsdp_id(fsdp_peer(o)) for o in FSDP_OFFSETS
    ]
    for peer in greeted:
        pl.semaphore_signal(barrier, inc=1, device_id=peer, device_id_type=MESH)

    def columns(s):
        return pl.ds(pl.multiple_of(s * HEAD, HEAD), HEAD)

    def chunk(s):
        return pl.ds(pl.multiple_of(s * IMAGE_CHUNK, IMAGE_CHUNK), IMAGE_CHUNK)

    def token_slot(p, r, h):
        start = ((p * 4 + r) * 2 + core) * IMAGE_CHUNK + h * half
        return tokens.at[pl.ds(pl.multiple_of(start, half), half), :]

    def weight_slot(p, r, h):
        start = (p * 4 + r) * WEIGHT_ROWS + h * whalf
        return weights.at[0, pl.ds(pl.multiple_of(start, whalf), whalf), :]

    group_rows = pl.ds(pl.multiple_of(group * WEIGHT_ROWS, WEIGHT_ROWS), WEIGHT_ROWS)
    fill_image = pltpu.make_async_copy(image, tokens.at[chunk(own), :], local_sems.at[0])
    fill_weights = [
        pltpu.make_async_copy(
            w_qkv.at[j, :, columns(own)],
            weights.at[0, group_rows, j * HEAD : (j + 1) * HEAD],
            local_sems.at[1 + j],
        )
        for j in range(3)
    ]
    fill_text = pltpu.make_async_copy(text, tokens.at[text_rows, :], local_sems.at[4])
    fill_upstream = [
        pltpu.make_async_copy(
            cotangent.at[:, columns(own)], upstream.at[chunk(own), :], local_sems.at[5]
        ),
        pltpu.make_async_copy(
            text_cotangent.at[:, columns(own)], upstream.at[text_rows, :], local_sems.at[6]
        ),
    ]
    for fill in (fill_image, *fill_weights, fill_text, *fill_upstream):
        fill.start()

    copies = Copies(send, recv)
    t = GatherRing(copies, token_slot, "seq_0", xh, "seq_1", z)
    w = GatherRing(copies, weight_slot, "fsdp_0", xl, "fsdp_1", y)
    shared = {}
    for plane, d in UNITS:
        for h in range(2):
            piece = token_slot(planes[plane], (z + d) % 4, h)
            shared[plane, d, h] = copies.make(piece, piece, other_core)
    exchanged = []
    for offset in SEQ_OFFSETS:
        peer = seq_peer(offset)
        s = (peer[0] * 4 + peer[1]) * 2 + peer[2]
        exchanged.append(
            copies.make(cotangent.at[:, columns(s)], upstream.at[chunk(own), :], seq_id(peer))
        )
    weights_shared = copies.make(weights.at[0], weights.at[1], other_core)

    def unit_at(plane, d):
        return planes[plane] * 4 + (z + d) % 4

    grads_shared = {}
    for plane, d in UNITS:
        at = unit_at(plane, d)
        grads_shared[plane, d] = copies.make(
            grads.at[chunk(at * 2 + 1 - core), :], grads_other.at[chunk(at), :], other_core
        )
    text_half = text_count // 2

    def text_share(c):
        return pl.ds(pl.multiple_of(IMAGE_ROWS + c * text_half, text_half), text_half)

    text_got = pl.ds(IMAGE_ROWS // 2, text_half)
    text_shared = copies.make(grads.at[text_share(1 - core), :], grads_other.at[text_got, :], other_core)
    gain_first = [
        copies.make(gain_seq.at[own], gain_seq.at[own], seq_id(seq_peer(o))) for o in SEQ_OFFSETS
    ]
    gain_second = [
        copies.make(gain_fsdp.at[group], gain_fsdp.at[group], fsdp_id(fsdp_peer(o)))
        for o in FSDP_OFFSETS
    ]
    text_first, text_second = [], []
    for o in FSDP_OFFSETS:
        peer = seq_peer((o[0], o[1], 0))
        to = {"seq_0": peer[0], "seq_1": peer[1]}
        text_first.append(copies.make(text_part.at[peer[0], peer[1]], text_in.at[xh, z], to))
        text_second.append(copies.make(text_all.at[core, xh, z], text_all.at[core, xh, z], to))
    text_third = copies.make(text_all.at[core], text_all.at[core], other_core)

    def dx_value(plane, d, h):
        start = (plane * 4 + d) * IMAGE_CHUNK + h * half
        return expd[start : start + half, : tokens.shape[1]]

    def dw_value(plane, d, h):
        f = (xl if plane == 0 else 1 - xl) * 4 + (y + d) % 4
        return dw[pl.ds(pl.multiple_of(f * WEIGHT_ROWS + h * whalf, whalf), whalf), :]

    dx_ring = ReduceRing(copies, dx_out, dx_in, dx_value, "seq_0", xh, "seq_1", z)
    dw_ring = ReduceRing(copies, dw_out, dw_in, dw_value, "fsdp_0", xl, "fsdp_1", y)

    fill_image.wait()
    pl.semaphore_wait(barrier, len(greeted))
    for h in range(2):
        t.cross[h].start()
        t.up[0][h].start()
        t.down[0][1 - h].start()
    for fill in fill_weights:
        fill.wait()
    for h in range(2):
        w.cross[h].start()
        w.up[0][h].start()
        w.down[0][1 - h].start()
    for h in range(2):
        shared[0, 0, h].start()

    t.up[0][0].wait_recv()
    t.pass_up.start()
    shared[0, 3, 0].start()
    t.down[0][1].wait_recv()
    t.pass_down.start()
    shared[0, 1, 1].start()
    w.up[0][0].wait_recv()
    w.pass_up.start()
    w.down[0][1].wait_recv()
    w.pass_down.start()
    for h in range(2):
        w.cross[h].wait_recv()
        w.up[1][h].start()
        w.down[1][h].start()
    for h in range(2):
        t.cross[h].wait_recv()
        t.up[1][h].start()
        t.down[1][h].start()
        shared[1, 0, h].start()
    t.up[0][1].wait_recv()
    shared[0, 3, 1].start()
    t.down[0][0].wait_recv()
    shared[0, 1, 0].start()
    w.pass_up.wait_recv()
    w.far[0].start()
    w.pass_down.wait_recv()
    w.far[1].start()
    t.pass_up.wait_recv()
    t.far[0].start()
    shared[0, 2, 0].start()
    t.pass_down.wait_recv()
    t.far[1].start()
    shared[0, 2, 1].start()
    for copy in exchanged:
        copy.start()
    w.up[0][1].wait_recv()
    w.down[0][0].wait_recv()
    for h in range(2):
        w.up[1][h].wait_recv()
        w.down[1][h].wait_recv()
        w.far[h].wait_recv()
    weights_shared.start()

    def normed(values, gain):
        inverse = lax.rsqrt(jnp.mean(values * values, axis=-1, keepdims=True) + EPS)
        return (values * inverse * gain).astype(BF16)

    def project(start, count):
        at = pl.ds(start, count)
        result = dot_nn(tokens[at, :], weights[0]).astype(BF16)
        triple[at, :] = result
        qn[at, :] = normed(result[:, :HEAD].astype(F32), qgain[...])
        keys = normed(result[:, HEAD : 2 * HEAD].astype(F32), kgain[...])
        kn[at, :] = keys
        kn_t[:, at] = keys.T

    def unit_start(plane, d):
        return pl.multiple_of(unit_at(plane, d) * Q_ROWS, Q_ROWS)

    def project_unit(plane, d):
        for h in range(2):
            shared[plane, d, h].wait_recv()
        project(unit_start(plane, d), Q_ROWS)

    fill_text.wait()
    project(IMAGE_ROWS, text_count)
    for d in range(4):
        project_unit(0, d)
    for h in range(2):
        t.up[1][h].wait_recv()
        shared[1, 3, h].start()
        t.down[1][h].wait_recv()
        shared[1, 1, h].start()
    project_unit(1, 0)
    for h in range(2):
        t.far[h].wait_recv()
        shared[1, 2, h].start()
    project_unit(1, 1)
    project_unit(1, 3)
    project_unit(1, 2)

    dv[...] = jnp.zeros_like(dv)
    gsum[...] = jnp.zeros_like(gsum)
    key_parts = [pl.ds(c, KEY_ROWS) for c in range(0, total_rows, KEY_ROWS)]

    def exponentials(start, count):
        at = pl.ds(start, count)
        qb = qn[at, :]
        total = jnp.zeros((8, count), F32)
        for part in key_parts:
            e = jnp.exp2(dot_nt(kn[part, :], qb) * scale)
            expd[part, at] = e
            total = total + folded(e)
        esum[:, at] = total

    def score_grads(start, count):
        at = pl.ds(start, count)
        ub = upstream[at, :]
        inner = jnp.zeros((8, count), F32)
        for part in key_parts:
            d = dot_nt(triple[part, 2 * HEAD :], ub)
            dpd[part, :count] = d
            inner = inner + folded(expd[part, at] * d)
        recip = 1.0 / jnp.sum(esum[:, at], axis=0, keepdims=True)
        delta = jnp.sum(inner, axis=0, keepdims=True) * recip
        for part in key_parts:
            p = expd[part, at] * recip
            dsd[part, at] = (p * (dpd[part, :count] - delta)).astype(BF16)
            dv[part, :] += dot_nn(p.astype(BF16), ub)

    def over_blocks(block):
        def step(i, carry):
            block(pl.multiple_of(i * Q_ROWS, Q_ROWS), Q_ROWS)
            return carry

        lax.fori_loop(0, IMAGE_ROWS // Q_ROWS, step, 0)
        block(IMAGE_ROWS, text_count)

    over_blocks(exponentials)
    for copy in exchanged:
        copy.wait_recv()
    for fill in fill_upstream:
        fill.wait()
    over_blocks(score_grads)

    def back(values, gain, incoming):
        floated = values.astype(F32)
        inverse = lax.rsqrt(jnp.mean(floated * floated, axis=-1, keepdims=True) + EPS)
        weighted = incoming * gain
        inner = jnp.mean(weighted * floated, axis=-1, keepdims=True)
        grad = inverse * weighted - floated * (inverse * inverse * inverse * inner)
        return grad.astype(BF16), folded(incoming * floated * inverse)

    def token_grads(start, count):
        at = pl.ds(start, count)
        dq = dot_nn(kn_t[...], dsd[:, at]).T * factor
        dk = dot_nn(dsd[at, :], qn[...]) * factor
        dq, q_part = back(triple[at, :HEAD], qgain[...], dq)
        dk, k_part = back(triple[at, HEAD : 2 * HEAD], kgain[...], dk)
        grads[at, :HEAD] = dq
        grads[at, HEAD : 2 * HEAD] = dk
        grads[at, 2 * HEAD :] = dv[at, :].astype(BF16)
        gsum[0:8, :] += q_part
        gsum[8:16, :] += k_part

    def unit_grads(plane, d):
        token_grads(unit_start(plane, d), Q_ROWS)
        grads_shared[plane, d].start()

    def input_part(mine, theirs):
        return dot_nt(grads[mine, :], weights[0]) + dot_nt(grads_other[theirs, :], weights[1])

    def input_sum(plane, d):
        at = unit_at(plane, d)
        grads_shared[plane, d].wait_recv()
        start = (plane * 4 + d) * IMAGE_CHUNK
        expd[start : start + IMAGE_CHUNK, : tokens.shape[1]] = input_part(
            chunk(at * 2 + core), chunk(at)
        )

    def weight_part(j):
        block = 2 * WEIGHT_ROWS
        dw[j * block : (j + 1) * block, :] = dot_tn(
            tokens[:, j * block : (j + 1) * block], grads[...]
        )

    unit_grads(1, 2)
    unit_grads(1, 1)
    weights_shared.wait_recv()
    input_sum(1, 2)
    dx_ring.send_far()
    unit_grads(1, 3)
    input_sum(1, 1)
    dx_ring.send_up()
    unit_grads(0, 2)
    input_sum(1, 3)
    dx_ring.send_down()
    unit_grads(0, 1)
    unit_grads(0, 3)
    input_sum(0, 1)
    dx_ring.own_up()
    input_sum(0, 3)
    dx_ring.own_down()
    input_sum(0, 2)
    dx_ring.own_far()
    token_grads(IMAGE_ROWS, text_count)
    text_shared.start()
    unit_grads(1, 0)
    unit_grads(0, 0)
    gain_seq[own] = jnp.zeros(gain_seq.shape[1:], F32)
    gain_seq[own, 0:1, :] = jnp.sum(gsum[0:8, :], axis=0, keepdims=True)
    gain_seq[own, 1:2, :] = jnp.sum(gsum[8:16, :], axis=0, keepdims=True)
    for copy in gain_first:
        copy.start()
    weight_part(0)
    weight_part(1)
    input_sum(1, 0)
    dx_ring.cross()
    dx_ring.pass_on()
    weight_part(2)
    weight_part(3)
    dw_ring.send_far()
    dw_ring.send_up()
    dw_ring.send_down()
    dw_ring.own_up()
    dw_ring.own_down()
    text_shared.wait_recv()
    text_sum = input_part(text_share(core), text_got).astype(BF16)
    rows, width = text_part.shape[2:]
    for a, b in UNITS:
        text_part[a, b] = text_sum[b * rows : (b + 1) * rows, a * width : (a + 1) * width]
    for copy in text_first:
        copy.start()
    text_in[xh, z] = text_part[xh, z]
    dw_ring.own_far()
    input_sum(0, 0)
    for copy in gain_first:
        copy.wait_recv()
    gain_fsdp[group] = jnp.sum(gain_seq[...], axis=0)
    for copy in gain_second:
        copy.start()
    dw_ring.cross()
    dw_ring.pass_on()
    for copy in text_first:
        copy.wait_recv()
    text_all[core, xh, z] = jnp.sum(text_in[...].astype(F32), axis=(0, 1)).astype(BF16)
    for copy in text_second:
        copy.start()
    for copy in gain_second:
        copy.wait_recv()
    gain_out[...] = jnp.sum(gain_fsdp[...], axis=0)[0:2]
    for copy in text_second:
        copy.wait_recv()
    text_third.start()
    for h in range(2):
        image_out[h * half : (h + 1) * half, :] = dx_ring.total(h).astype(BF16)
    for h in range(2):
        total = dw_ring.total(h)
        for j in range(3):
            weight_out[j, h * whalf : (h + 1) * whalf, :] = total[:, j * HEAD : (j + 1) * HEAD]
    text_third.wait_recv()
    for c in range(2):
        for a, b in UNITS:
            text_out[
                c * text_half + b * rows : c * text_half + (b + 1) * rows,
                a * width : (a + 1) * width,
            ] = text_all[c, a, b]
    for copy in copies.made:
        copy.wait_send()


def step(image, text, w_qkv, query_gain, key_gain, cotangent, text_cotangent):
    features = image.shape[1]
    text_count = text.shape[0]
    total = IMAGE_ROWS + text_count
    depth = w_qkv.shape[1] * 8
    hbm = pl.BlockSpec(memory_space=pltpu.HBM)
    vmem = pl.BlockSpec(memory_space=pltpu.VMEM)
    half, whalf = IMAGE_CHUNK // 2, WEIGHT_ROWS // 2
    text_piece = (2, 4, text_count // 8, features // 2)
    n_copies = (
        2 * GATHER_COPIES + 16 + len(SEQ_OFFSETS) + 1 + 9
        + len(SEQ_OFFSETS) + len(FSDP_OFFSETS) + 2 * len(FSDP_OFFSETS) + 1 + 2 * REDUCE_COPIES
    )
    return pl.pallas_call(
        step_kernel,
        out_shape=(
            jax.ShapeDtypeStruct((IMAGE_CHUNK, features), BF16),
            jax.ShapeDtypeStruct((text_count, features), BF16),
            jax.ShapeDtypeStruct((3, WEIGHT_ROWS, HEAD), F32),
            jax.ShapeDtypeStruct((2, HEAD), F32),
        ),
        in_specs=[hbm, hbm, hbm, vmem, vmem, hbm, hbm],
        out_specs=(vmem,) * 4,
        scratch_shapes=[
            pltpu.VMEM((total, features), BF16),
            pltpu.VMEM((2, depth, WIDTH), BF16),
            pltpu.VMEM((total, WIDTH), BF16),
            pltpu.VMEM((total, HEAD), BF16),
            pltpu.VMEM((total, HEAD), BF16),
            pltpu.VMEM((total, HEAD), BF16),
            pltpu.VMEM((HEAD, total), BF16),
            pltpu.VMEM((total, total), F32),
            pltpu.VMEM((8, total), F32),
            pltpu.VMEM((total, total), BF16),
            pltpu.VMEM((total, Q_ROWS), F32),
            pltpu.VMEM((total, HEAD), F32),
            pltpu.VMEM((16, HEAD), F32),
            pltpu.VMEM((total, WIDTH), BF16),
            pltpu.VMEM((total // 2, WIDTH), BF16),
            pltpu.VMEM((depth, WIDTH), F32),
            pltpu.VMEM((REDUCE_COPIES, half, features), BF16),
            pltpu.VMEM((REDUCE_COPIES, half, features), BF16),
            pltpu.VMEM((REDUCE_COPIES, whalf, WIDTH), BF16),
            pltpu.VMEM((REDUCE_COPIES, whalf, WIDTH), BF16),
            pltpu.VMEM(text_piece, BF16),
            pltpu.VMEM(text_piece, BF16),
            pltpu.VMEM((2, *text_piece), BF16),
            pltpu.VMEM((16, 8, HEAD), F32),
            pltpu.VMEM((8, 8, HEAD), F32),
            pltpu.SemaphoreType.DMA((n_copies,)),
            pltpu.SemaphoreType.DMA((n_copies,)),
            pltpu.SemaphoreType.DMA((7,)),
        ],
        compiler_params=pltpu.CompilerParams(
            collective_id=0, has_side_effects=True, vmem_limit_bytes=62 * 1024 * 1024
        ),
        name="step",
    )(image, text, w_qkv, query_gain, key_gain, cotangent, text_cotangent)


def store_kernel(*refs):
    count = (len(refs) - 1) // 2
    sems = refs[-1]
    moves = [
        pltpu.make_async_copy(refs[i], refs[count + i], sems.at[i]) for i in range(count)
    ]
    for move in moves:
        move.start()
    for move in moves:
        move.wait()


def store(*arrays):
    hbm = pl.BlockSpec(memory_space=pltpu.HBM)
    vmem = pl.BlockSpec(memory_space=pltpu.VMEM)
    return pl.pallas_call(
        store_kernel,
        out_shape=tuple(jax.ShapeDtypeStruct(a.shape, a.dtype) for a in arrays),
        in_specs=[vmem] * len(arrays),
        out_specs=(hbm,) * len(arrays),
        scratch_shapes=[pltpu.SemaphoreType.DMA((len(arrays),))],
        compiler_params=pltpu.CompilerParams(vmem_limit_bytes=4 * 1024 * 1024),
        name="store",
    )(*arrays)


def local(image_input, text_input, w_qkv, query_gain, key_gain, image_cotangent, text_cotangent):
    image_out, text_out, grad_weights, gain_total = store(
        *step(
            image_input[0],
            text_input[0],
            w_qkv.transpose(1, 0, 2),
            query_gain.reshape(1, HEAD),
            key_gain.reshape(1, HEAD),
            image_cotangent[0],
            text_cotangent[0],
        )
    )
    return image_out[None], text_out[None], grad_weights.transpose(1, 0, 2), gain_total


def solution(mesh):
    finer = Mesh(
        mesh.devices.reshape(2, 4, 2, 4, 2), ("fsdp_0", "fsdp_1", "seq_0", "seq_1", "seq_2")
    )
    return jax.shard_map(
        local,
        mesh=finer,
        in_specs=(
            P(FSDP, SEQ, None),
            P(FSDP, None, None),
            P(FSDP, None, None),
            P(),
            P(),
            P(FSDP, SEQ, None),
            P(FSDP, None, None),
        ),
        out_specs=(P(FSDP, SEQ, None), P(FSDP, None, None), P(FSDP, None, SEQ), P()),
        check_vma=False,
    )
```

time: 434 us -> 107 us (0.25)
  waiting for transfers between devices: 289 us -> 0 us
  Pallas kernels: 19.1 us -> 102 us
  blocking collectives: 64.8 us -> 0 us
  matrix products: 17 us -> 0 us
  local copies, waits for them, and re-layouts: 17.5 us -> 3.61 us
  between operations: 13.9 us -> 0.83 us
  starting transfers between devices: 9.66 us -> 0 us
    psum x1 -> x0, waiting for transfers between devices: 97.1 us -> none  [local(): text_out = lax.psum(partial[image_rows:], SEQ)]
    reduce_scatter x2 -> x0, waiting for transfers between devices: 94.2 us -> none  [the longest x1 94.2 us: local(): lax.psum_scatter(partial[:image_rows], SEQ, scatter_dimension=0, tiled=True)]
    all_gather x2 -> x0, waiting for transfers between devices: 82.9 us -> none  [the longest x1 71.2 us: local(): whole_image = lax.all_gather(image_input[0], SEQ, axis=0, tiled=True)]
    pallas_call x1 -> x2, Pallas kernels: 19.1 us -> 102 us  [the longest x1 101 us: step(): pl.pallas_call(step_kernel, out_shape=(jax.ShapeDtypeStruct((IMAGE_CHUNK,...]
    psum x1 -> x0, blocking collectives: 64.8 us -> none  [local(): gain_total = lax.psum(gain_part, FSDP_SEQ)]
    dot_general x3 -> x0, matrix products: 17 us -> none  [the longest x1 6.86 us: local(): triple = jnp.dot(tokens, weights, preferred_element_type=F32).astype(BF16)]
    all_to_all x1 -> x0, waiting for transfers between devices: 14.3 us -> none  [local(): lax.all_to_all(image_cotangent[0], SEQ, split_axis=1, concat_axis=0, tile...]
    all_to_all x1 -> x0, starting transfers between devices: 9.28 us -> none  [local(): lax.all_to_all(image_cotangent[0], SEQ, split_axis=1, concat_axis=0, tile...]
  transfers between devices with their start and end apart: 6 -> 0, of which waited for: 5 -> 0; matrix products, arithmetic and copies ran while one was open for 4% -> 0% of each run, Pallas kernels for 0% -> 0%
where the time goes in v4:
time: 107 us; the launch traced here: 106 us
  Pallas kernels  102 us (95%)
  local copies, waits for them, and re-layouts  3.61 us (3%)
    pallas_call x1, Pallas kernels, step(): pl.pallas_call(step_kernel, out_shape=(jax.ShapeDtypeStruct((IMAGE_CHUNK,...  101 us
    unnamed x8, local copies, waits for them, and re-layouts  3.61 us

profile of v4, /device:TPU:1, one launch (start us, length us, event | category | flops | bytes accessed | tf_op | source)
XLA Modules:
  0.0 106.3 jit_solution(12106531504489537093)
XLA Ops:
  0.6 100.9 %step.1 = (bf16[128,1536]{1,0:T(8,128)(2,1)}, bf16[128,1536]{1,0:T(8,128)(2,1)}, f32[3,192,128]{2,1,0:T(8,128)}, f32[2,128]{1,0:T(2,128)}) custom-call(bf16[128,1536]{1,0:T(8,128)(2,1)} %bitcast.13, bf16[128,1536]{1,0:T(8,128)(2,1)} %bitcast.14, bf16[3,192,2048]{2,1,0:T(8,128)(2,1)} %bitcast.10, f32[1,128]{1,0:T(1,128)} %bitcast.15, f32[1,128]{1,0:T(1,128)} %bitcast.16, ...), custom_call_target="tpu_custom_call" | custom-call | tf_op jit(solution)/shard_map/step/pallas_call | solution.py:573
  101.5 0.0 copy-start
  101.5 1.0 copy-done
  102.5 0.0 copy-start.1
  102.5 1.0 copy-done.1
  103.5 0.0 copy-start.2
  103.5 1.0 copy-done.2
  104.5 0.0 copy-start.3
  104.5 0.7 copy-done.3
  105.1 1.0 store.1
Async XLA Ops:
  101.5 1.0 copy-start
  102.5 1.0 copy-start.1
  103.5 1.0 copy-start.2
  104.5 0.7 copy-start.3

commit v5 on v4

--- a/solution.py
+++ b/solution.py
@@ -146,13 +146,11 @@
     def own_down(self):
         self.put(10, self.value(0, 3, 0))
 
-    def own_far(self):
-        self.put(6, self.value(0, 2, 0) + self.got(0))
-        self.put(9, self.value(0, 2, 1) + self.got(1))
-
-    def pass_on(self):
-        self.put(8, self.value(0, 1, 0) + self.got(6))
-        self.put(11, self.value(0, 3, 1) + self.got(9))
+    def own_far(self, h):
+        self.put((6, 9)[h], self.value(0, 2, h) + self.got(h))
+
+    def pass_on(self, h):
+        self.put((8, 11)[h], self.value(0, (1, 3)[h], h) + self.got((6, 9)[h]))
 
     def cross(self):
         self.put(12, self.value(1, 0, 0) + self.got(2) + self.got(4))
@@ -416,20 +414,31 @@
             dsd[part, at] = (p * (dpd[part, :count] - delta)).astype(BF16)
             dv[part, :] += dot_nn(p.astype(BF16), ub)
 
-    def over_blocks(block):
-        def step(i, carry):
-            block(pl.multiple_of(i * Q_ROWS, Q_ROWS), Q_ROWS)
-            return carry
-
-        lax.fori_loop(0, IMAGE_ROWS // Q_ROWS, step, 0)
-        block(IMAGE_ROWS, text_count)
-
-    over_blocks(exponentials)
-    for copy in exchanged:
-        copy.wait_recv()
+    def exponential_block(i, carry):
+        exponentials(pl.multiple_of(i * Q_ROWS, Q_ROWS), Q_ROWS)
+        return carry
+
+    blocks = IMAGE_ROWS // Q_ROWS
+    lax.fori_loop(0, blocks, exponential_block, 0)
+    exponentials(IMAGE_ROWS, text_count)
     for fill in fill_upstream:
         fill.wait()
-    over_blocks(score_grads)
+    score_grads(IMAGE_ROWS, text_count)
+
+    def score_block(i, carry):
+        for plane in range(2):
+
+            @pl.when(i == 4 * plane)
+            def _():
+                for offset, copy in zip(SEQ_OFFSETS, exchanged):
+                    if offset[0] == plane:
+                        copy.wait_recv()
+
+        at = (xh + i // 4) % 2 * 4 + (z + i) % 4
+        score_grads(pl.multiple_of(at * Q_ROWS, Q_ROWS), Q_ROWS)
+        return carry
+
+    lax.fori_loop(0, blocks, score_block, 0)
 
     def back(values, gain, incoming):
         floated = values.astype(F32)
@@ -472,39 +481,34 @@
             tokens[:, j * block : (j + 1) * block], grads[...]
         )
 
+    unit_grads(1, 1)
     unit_grads(1, 2)
-    unit_grads(1, 1)
+    unit_grads(1, 3)
     weights_shared.wait_recv()
+    input_sum(1, 1)
+    dx_ring.send_up()
     input_sum(1, 2)
     dx_ring.send_far()
-    unit_grads(1, 3)
-    input_sum(1, 1)
-    dx_ring.send_up()
-    unit_grads(0, 2)
     input_sum(1, 3)
     dx_ring.send_down()
-    unit_grads(0, 1)
-    unit_grads(0, 3)
-    input_sum(0, 1)
-    dx_ring.own_up()
-    input_sum(0, 3)
-    dx_ring.own_down()
-    input_sum(0, 2)
-    dx_ring.own_far()
+    for unit in ((0, 2), (0, 1), (0, 3), (1, 0), (0, 0)):
+        unit_grads(*unit)
     token_grads(IMAGE_ROWS, text_count)
     text_shared.start()
-    unit_grads(1, 0)
-    unit_grads(0, 0)
     gain_seq[own] = jnp.zeros(gain_seq.shape[1:], F32)
     gain_seq[own, 0:1, :] = jnp.sum(gsum[0:8, :], axis=0, keepdims=True)
     gain_seq[own, 1:2, :] = jnp.sum(gsum[8:16, :], axis=0, keepdims=True)
     for copy in gain_first:
         copy.start()
+    input_sum(0, 2)
+    dx_ring.own_far(0)
     weight_part(0)
     weight_part(1)
-    input_sum(1, 0)
-    dx_ring.cross()
-    dx_ring.pass_on()
+    input_sum(0, 1)
+    dx_ring.own_up()
+    dx_ring.own_far(1)
+    input_sum(0, 3)
+    dx_ring.own_down()
     weight_part(2)
     weight_part(3)
     dw_ring.send_far()
@@ -512,6 +516,8 @@
     dw_ring.send_down()
     dw_ring.own_up()
     dw_ring.own_down()
+    input_sum(1, 0)
+    dx_ring.cross()
     text_shared.wait_recv()
     text_sum = input_part(text_share(core), text_got).astype(BF16)
     rows, width = text_part.shape[2:]
@@ -520,20 +526,24 @@
     for copy in text_first:
         copy.start()
     text_in[xh, z] = text_part[xh, z]
-    dw_ring.own_far()
+    dx_ring.pass_on(0)
     input_sum(0, 0)
     for copy in gain_first:
         copy.wait_recv()
     gain_fsdp[group] = jnp.sum(gain_seq[...], axis=0)
     for copy in gain_second:
         copy.start()
+    for h in range(2):
+        dw_ring.own_far(h)
+    dx_ring.pass_on(1)
     dw_ring.cross()
-    dw_ring.pass_on()
     for copy in text_first:
         copy.wait_recv()
     text_all[core, xh, z] = jnp.sum(text_in[...].astype(F32), axis=(0, 1)).astype(BF16)
     for copy in text_second:
         copy.start()
+    for h in range(2):
+        dw_ring.pass_on(h)
     for copy in gain_second:
         copy.wait_recv()
     gain_out[...] = jnp.sum(gain_fsdp[...], axis=0)[0:2]
@@ -618,27 +628,30 @@
 
 
 def store_kernel(*refs):
-    count = (len(refs) - 1) // 2
-    sems = refs[-1]
-    moves = [
-        pltpu.make_async_copy(refs[i], refs[count + i], sems.at[i]) for i in range(count)
-    ]
-    for move in moves:
-        move.start()
-    for move in moves:
-        move.wait()
+    count = (len(refs) - 2) // 3
+    taken, kept, held = refs[:count], refs[count : 2 * count], refs[2 * count : 3 * count]
+    loads, stores = refs[-2:]
+    ins = [pltpu.make_async_copy(taken[i], held[i], loads.at[i]) for i in range(count)]
+    outs = [pltpu.make_async_copy(held[i], kept[i], stores.at[i]) for i in range(count)]
+    for copy in ins:
+        copy.start()
+    for i in range(count):
+        ins[i].wait()
+        outs[i].start()
+    for copy in outs:
+        copy.wait()
 
 
 def store(*arrays):
     hbm = pl.BlockSpec(memory_space=pltpu.HBM)
-    vmem = pl.BlockSpec(memory_space=pltpu.VMEM)
     return pl.pallas_call(
         store_kernel,
         out_shape=tuple(jax.ShapeDtypeStruct(a.shape, a.dtype) for a in arrays),
-        in_specs=[vmem] * len(arrays),
+        in_specs=[hbm] * len(arrays),
         out_specs=(hbm,) * len(arrays),
-        scratch_shapes=[pltpu.SemaphoreType.DMA((len(arrays),))],
-        compiler_params=pltpu.CompilerParams(vmem_limit_bytes=4 * 1024 * 1024),
+        scratch_shapes=[pltpu.VMEM(a.shape, a.dtype) for a in arrays]
+        + [pltpu.SemaphoreType.DMA((len(arrays),))] * 2,
+        compiler_params=pltpu.CompilerParams(vmem_limit_bytes=67043328),
         name="store",
     )(*arrays)
 

time: 107 us -> 102 us (0.953)
  local copies, waits for them, and re-layouts: 3.61 us -> 0 us
    unnamed x8 -> x0, local copies, waits for them, and re-layouts: 3.61 us -> none
    pallas_call x1, Pallas kernels: 101 us -> 98.6 us  [step(): pl.pallas_call(step_kernel, out_shape=(jax.ShapeDtypeStruct((IMAGE_CHUNK,...]
where the time goes in v5:
time: 102 us; the launch traced here: 101 us
  Pallas kernels  101 us (99%)
    pallas_call x1, Pallas kernels, step(): pl.pallas_call(step_kernel, out_shape=(jax.ShapeDtypeStruct((IMAGE_CHUNK,...  98.6 us
    pallas_call x1, Pallas kernels, store(): pl.pallas_call(store_kernel, out_shape=tuple((jax.ShapeDtypeStruct(a.shap...  2.04 us

profile of v5, /device:TPU:1, one launch (start us, length us, event | category | flops | bytes accessed | tf_op | source)
XLA Modules:
  0.0 101.5 jit_solution(8835978154366813403)
XLA Ops:
  0.6 98.6 %step.1 = (bf16[128,1536]{1,0:T(8,128)(2,1)}, bf16[128,1536]{1,0:T(8,128)(2,1)}, f32[3,192,128]{2,1,0:T(8,128)}, f32[2,128]{1,0:T(2,128)}) custom-call(bf16[128,1536]{1,0:T(8,128)(2,1)} %bitcast.13, bf16[128,1536]{1,0:T(8,128)(2,1)} %bitcast.14, bf16[3,192,2048]{2,1,0:T(8,128)(2,1)} %bitcast.10, f32[1,128]{1,0:T(1,128)} %bitcast.15, f32[1,128]{1,0:T(1,128)} %bitcast.16, ...), custom_call_target="tpu_custom_call" | custom-call | tf_op jit(solution)/shard_map/step/pallas_call | solution.py:583
  99.3 2.0 %store.1 = (bf16[128,1536]{1,0:T(8,128)(2,1)}, bf16[128,1536]{1,0:T(8,128)(2,1)}, f32[3,192,128]{2,1,0:T(8,128)}, f32[2,128]{1,0:T(2,128)}) custom-call(bf16[128,1536]{1,0:T(8,128)(2,1)} %get-tuple-element.12.refs_0_, bf16[128,1536]{1,0:T(8,128)(2,1)} %get-tuple-element.13.refs_1_, f32[3,192,128]{2,1,0:T(8,128)} %get-tuple-element.14.refs_2_, ...), custom_call_target="tpu_custom_call" | custom-call | tf_op jit(solution)/shard_map/store/pallas_call | solution.py:647

commit v6 on v5

--- a/solution.py
+++ b/solution.py
@@ -93,7 +93,7 @@
 
 
 class GatherRing:
-    def __init__(self, copies, slot, pair_axis, pair, ring_axis, ring):
+    def __init__(self, copies, slot, pair_axis, pair, ring_axis, ring, far):
         self.planes = (pair, 1 - pair)
         after, before = {ring_axis: (ring + 1) % 4}, {ring_axis: (ring + 3) % 4}
         other = {pair_axis: 1 - pair}
@@ -104,9 +104,11 @@
         self.cross = [same(slot(pair, ring, h), other) for h in range(2)]
         self.up = [[same(slot(p, ring, h), after) for h in range(2)] for p in self.planes]
         self.down = [[same(slot(p, ring, h), before) for h in range(2)] for p in self.planes]
-        self.pass_up = same(slot(pair, (ring + 3) % 4, 0), after)
-        self.pass_down = same(slot(pair, (ring + 1) % 4, 1), before)
-        self.far = [same(slot(pair, (ring + 2) % 4, h), other) for h in range(2)]
+        passed = self.planes[:1] if far else self.planes
+        self.pass_up = [same(slot(p, (ring + 3) % 4, 0), after) for p in passed]
+        self.pass_down = [same(slot(p, (ring + 1) % 4, 1), before) for p in passed]
+        if far:
+            self.far = [same(slot(pair, (ring + 2) % 4, h), other) for h in range(2)]
 
 
 GATHER_COPIES = 14
@@ -162,6 +164,38 @@
         for i in parts:
             result = result + self.got(i)
         return result
+
+
+class PlainReduceRing(ReduceRing):
+    def __init__(self, copies, out, arrived, value, pair_axis, pair, ring_axis, ring):
+        up, down = {ring_axis: (ring + 1) % 4}, {ring_axis: (ring + 3) % 4}
+        to = ([up] * 3 + [down] * 3) * 2 + [{pair_axis: 1 - pair}] * 2
+        self.out, self.arrived, self.value = out, arrived, value
+        self.pieces = [copies.make(out.at[i], arrived.at[i], t) for i, t in enumerate(to)]
+
+    def first(self, plane):
+        base = 6 * (1 - plane)
+        self.put(base, self.value(plane, 2, 0))
+        self.put(base + 3, self.value(plane, 2, 1))
+        self.put(base + 1, self.value(plane, 1, 1))
+        self.put(base + 4, self.value(plane, 3, 0))
+
+    def pass_on(self, plane):
+        base = 6 * (1 - plane)
+        self.put(base + 2, self.value(plane, 1, 0) + self.got(base))
+        self.put(base + 5, self.value(plane, 3, 1) + self.got(base + 3))
+
+    def own(self, plane, h):
+        base = 6 * (1 - plane)
+        near = self.got(base + (2, 1)[h]) + self.got(base + (4, 5)[h])
+        return self.value(plane, 0, h) + near
+
+    def cross(self):
+        for h in range(2):
+            self.put(12 + h, self.own(1, h))
+
+    def total(self, h):
+        return self.own(0, h) + self.got(12 + h)
 
 
 REDUCE_COPIES = 14
@@ -231,8 +265,8 @@
         fill.start()
 
     copies = Copies(send, recv)
-    t = GatherRing(copies, token_slot, "seq_0", xh, "seq_1", z)
-    w = GatherRing(copies, weight_slot, "fsdp_0", xl, "fsdp_1", y)
+    t = GatherRing(copies, token_slot, "seq_0", xh, "seq_1", z, True)
+    w = GatherRing(copies, weight_slot, "fsdp_0", xl, "fsdp_1", y, False)
     shared = {}
     for plane, d in UNITS:
         for h in range(2):
@@ -287,7 +321,7 @@
         return dw[pl.ds(pl.multiple_of(f * WEIGHT_ROWS + h * whalf, whalf), whalf), :]
 
     dx_ring = ReduceRing(copies, dx_out, dx_in, dx_value, "seq_0", xh, "seq_1", z)
-    dw_ring = ReduceRing(copies, dw_out, dw_in, dw_value, "fsdp_0", xl, "fsdp_1", y)
+    dw_ring = PlainReduceRing(copies, dw_out, dw_in, dw_value, "fsdp_0", xl, "fsdp_1", y)
 
     fill_image.wait()
     pl.semaphore_wait(barrier, len(greeted))
@@ -304,16 +338,19 @@
     for h in range(2):
         shared[0, 0, h].start()
 
+    def pass_weights(plane):
+        w.up[plane][0].wait_recv()
+        w.pass_up[plane].start()
+        w.down[plane][1].wait_recv()
+        w.pass_down[plane].start()
+
     t.up[0][0].wait_recv()
-    t.pass_up.start()
+    t.pass_up[0].start()
     shared[0, 3, 0].start()
     t.down[0][1].wait_recv()
-    t.pass_down.start()
+    t.pass_down[0].start()
     shared[0, 1, 1].start()
-    w.up[0][0].wait_recv()
-    w.pass_up.start()
-    w.down[0][1].wait_recv()
-    w.pass_down.start()
+    pass_weights(0)
     for h in range(2):
         w.cross[h].wait_recv()
         w.up[1][h].start()
@@ -327,24 +364,20 @@
     shared[0, 3, 1].start()
     t.down[0][0].wait_recv()
     shared[0, 1, 0].start()
-    w.pass_up.wait_recv()
-    w.far[0].start()
-    w.pass_down.wait_recv()
-    w.far[1].start()
-    t.pass_up.wait_recv()
+    pass_weights(1)
+    t.pass_up[0].wait_recv()
     t.far[0].start()
     shared[0, 2, 0].start()
-    t.pass_down.wait_recv()
+    t.pass_down[0].wait_recv()
     t.far[1].start()
     shared[0, 2, 1].start()
     for copy in exchanged:
         copy.start()
-    w.up[0][1].wait_recv()
-    w.down[0][0].wait_recv()
-    for h in range(2):
-        w.up[1][h].wait_recv()
-        w.down[1][h].wait_recv()
-        w.far[h].wait_recv()
+    for plane in range(2):
+        w.up[plane][1].wait_recv()
+        w.down[plane][0].wait_recv()
+        w.pass_up[plane].wait_recv()
+        w.pass_down[plane].wait_recv()
     weights_shared.start()
 
     def normed(values, gain):
@@ -368,10 +401,39 @@
             shared[plane, d, h].wait_recv()
         project(unit_start(plane, d), Q_ROWS)
 
+    blocks = IMAGE_ROWS // Q_ROWS
+
+    def exponentials(start, count, keys):
+        at = pl.ds(start, count)
+        qb = qn[at, :]
+        total = jnp.zeros((8, count), F32)
+        for key in keys:
+            part = pl.ds(key, HEAD)
+            e = jnp.exp2(dot_nt(kn[part, :], qb) * scale)
+            expd[part, at] = e
+            total = total + folded(e)
+        esum[:, at] += total
+
+    def plane_keys(plane):
+        base = planes[plane] * (IMAGE_ROWS // 2)
+        return [pl.multiple_of(base + c, HEAD) for c in range(0, IMAGE_ROWS // 2, HEAD)]
+
+    def exponential_blocks(plane, keys):
+        def block(i, carry):
+            at = planes[plane] * (blocks // 2) + i
+            exponentials(pl.multiple_of(at * Q_ROWS, Q_ROWS), Q_ROWS, keys)
+            return carry
+
+        lax.fori_loop(0, blocks // 2, block, 0)
+
+    esum[...] = jnp.zeros_like(esum)
     fill_text.wait()
     project(IMAGE_ROWS, text_count)
     for d in range(4):
         project_unit(0, d)
+    own_keys = plane_keys(0) + [IMAGE_ROWS]
+    exponential_blocks(0, own_keys)
+    exponentials(IMAGE_ROWS, text_count, own_keys)
     for h in range(2):
         t.up[1][h].wait_recv()
         shared[1, 3, h].start()
@@ -385,19 +447,13 @@
     project_unit(1, 3)
     project_unit(1, 2)
 
+    exponential_blocks(1, plane_keys(0) + plane_keys(1) + [IMAGE_ROWS])
+    exponential_blocks(0, plane_keys(1))
+    exponentials(IMAGE_ROWS, text_count, plane_keys(1))
+
     dv[...] = jnp.zeros_like(dv)
     gsum[...] = jnp.zeros_like(gsum)
     key_parts = [pl.ds(c, KEY_ROWS) for c in range(0, total_rows, KEY_ROWS)]
-
-    def exponentials(start, count):
-        at = pl.ds(start, count)
-        qb = qn[at, :]
-        total = jnp.zeros((8, count), F32)
-        for part in key_parts:
-            e = jnp.exp2(dot_nt(kn[part, :], qb) * scale)
-            expd[part, at] = e
-            total = total + folded(e)
-        esum[:, at] = total
 
     def score_grads(start, count):
         at = pl.ds(start, count)
@@ -414,13 +470,6 @@
             dsd[part, at] = (p * (dpd[part, :count] - delta)).astype(BF16)
             dv[part, :] += dot_nn(p.astype(BF16), ub)
 
-    def exponential_block(i, carry):
-        exponentials(pl.multiple_of(i * Q_ROWS, Q_ROWS), Q_ROWS)
-        return carry
-
-    blocks = IMAGE_ROWS // Q_ROWS
-    lax.fori_loop(0, blocks, exponential_block, 0)
-    exponentials(IMAGE_ROWS, text_count)
     for fill in fill_upstream:
         fill.wait()
     score_grads(IMAGE_ROWS, text_count)
@@ -483,6 +532,8 @@
 
     unit_grads(1, 1)
     unit_grads(1, 2)
+    token_grads(IMAGE_ROWS, text_count)
+    text_shared.start()
     unit_grads(1, 3)
     weights_shared.wait_recv()
     input_sum(1, 1)
@@ -491,10 +542,16 @@
     dx_ring.send_far()
     input_sum(1, 3)
     dx_ring.send_down()
+    text_shared.wait_recv()
+    text_sum = input_part(text_share(core), text_got).astype(BF16)
+    rows, width = text_part.shape[2:]
+    for a, b in UNITS:
+        text_part[a, b] = text_sum[b * rows : (b + 1) * rows, a * width : (a + 1) * width]
+    for copy in text_first:
+        copy.start()
+    text_in[xh, z] = text_part[xh, z]
     for unit in ((0, 2), (0, 1), (0, 3), (1, 0), (0, 0)):
         unit_grads(*unit)
-    token_grads(IMAGE_ROWS, text_count)
-    text_shared.start()
     gain_seq[own] = jnp.zeros(gain_seq.shape[1:], F32)
     gain_seq[own, 0:1, :] = jnp.sum(gsum[0:8, :], axis=0, keepdims=True)
     gain_seq[own, 1:2, :] = jnp.sum(gsum[8:16, :], axis=0, keepdims=True)
@@ -511,39 +568,26 @@
     dx_ring.own_down()
     weight_part(2)
     weight_part(3)
-    dw_ring.send_far()
-    dw_ring.send_up()
-    dw_ring.send_down()
-    dw_ring.own_up()
-    dw_ring.own_down()
+    dw_ring.first(1)
     input_sum(1, 0)
     dx_ring.cross()
-    text_shared.wait_recv()
-    text_sum = input_part(text_share(core), text_got).astype(BF16)
-    rows, width = text_part.shape[2:]
-    for a, b in UNITS:
-        text_part[a, b] = text_sum[b * rows : (b + 1) * rows, a * width : (a + 1) * width]
+    dw_ring.first(0)
+    dx_ring.pass_on(0)
     for copy in text_first:
+        copy.wait_recv()
+    text_all[core, xh, z] = jnp.sum(text_in[...].astype(F32), axis=(0, 1)).astype(BF16)
+    for copy in text_second:
         copy.start()
-    text_in[xh, z] = text_part[xh, z]
-    dx_ring.pass_on(0)
-    input_sum(0, 0)
+    dw_ring.pass_on(1)
     for copy in gain_first:
         copy.wait_recv()
     gain_fsdp[group] = jnp.sum(gain_seq[...], axis=0)
     for copy in gain_second:
         copy.start()
-    for h in range(2):
-        dw_ring.own_far(h)
     dx_ring.pass_on(1)
+    dw_ring.pass_on(0)
     dw_ring.cross()
-    for copy in text_first:
-        copy.wait_recv()
-    text_all[core, xh, z] = jnp.sum(text_in[...].astype(F32), axis=(0, 1)).astype(BF16)
-    for copy in text_second:
-        copy.start()
-    for h in range(2):
-        dw_ring.pass_on(h)
+    input_sum(0, 0)
     for copy in gain_second:
         copy.wait_recv()
     gain_out[...] = jnp.sum(gain_fsdp[...], axis=0)[0:2]

time: 102 us -> 96.9 us (0.950)
  Pallas kernels: 101 us -> 95.9 us
    pallas_call x1, Pallas kernels: 98.6 us -> 93.8 us  [step(): pl.pallas_call(step_kernel, out_shape=(jax.ShapeDtypeStruct((IMAGE_CHUNK,...]
where the time goes in v6:
time: 96.9 us; the launch traced here: 96.7 us
  Pallas kernels  95.9 us (99%)
    pallas_call x1, Pallas kernels, step(): pl.pallas_call(step_kernel, out_shape=(jax.ShapeDtypeStruct((IMAGE_CHUNK,...  93.8 us
    pallas_call x1, Pallas kernels, store(): pl.pallas_call(store_kernel, out_shape=tuple((jax.ShapeDtypeStruct(a.shap...  2.04 us

profile of v6, /device:TPU:1, one launch (start us, length us, event | category | flops | bytes accessed | tf_op | source)
XLA Modules:
  0.0 96.7 jit_solution(13487462864018740039)
XLA Ops:
  0.6 93.8 %step.1 = (bf16[128,1536]{1,0:T(8,128)(2,1)}, bf16[128,1536]{1,0:T(8,128)(2,1)}, f32[3,192,128]{2,1,0:T(8,128)}, f32[2,128]{1,0:T(2,128)}) custom-call(bf16[128,1536]{1,0:T(8,128)(2,1)} %bitcast.13, bf16[128,1536]{1,0:T(8,128)(2,1)} %bitcast.14, bf16[3,192,2048]{2,1,0:T(8,128)(2,1)} %bitcast.10, f32[1,128]{1,0:T(1,128)} %bitcast.15, f32[1,128]{1,0:T(1,128)} %bitcast.16, ...), custom_call_target="tpu_custom_call" | custom-call | tf_op jit(solution)/shard_map/step/pallas_call | solution.py:627
  94.5 2.0 %store.1 = (bf16[128,1536]{1,0:T(8,128)(2,1)}, bf16[128,1536]{1,0:T(8,128)(2,1)}, f32[3,192,128]{2,1,0:T(8,128)}, f32[2,128]{1,0:T(2,128)}) custom-call(bf16[128,1536]{1,0:T(8,128)(2,1)} %get-tuple-element.12.refs_0_, bf16[128,1536]{1,0:T(8,128)(2,1)} %get-tuple-element.13.refs_1_, f32[3,192,128]{2,1,0:T(8,128)} %get-tuple-element.14.refs_2_, ...), custom_call_target="tpu_custom_call" | custom-call | tf_op jit(solution)/shard_map/store/pallas_call | solution.py:691

commit v7 on v6

--- a/solution.py
+++ b/solution.py
@@ -17,7 +17,7 @@
 MESH = pl.DeviceIdType.MESH
 
 Q_ROWS = 256
-KEY_ROWS = 136
+KEY_ROWS = 544
 IMAGE_CHUNK = 128
 IMAGE_ROWS = 2048
 WEIGHT_ROWS = 192
@@ -206,7 +206,7 @@
     image_out, text_out, weight_out, gain_out,
     tokens, weights, triple, upstream, qn, kn, kn_t, expd, esum, dsd, dpd, dv, gsum,
     grads, grads_other, dw, dx_out, dx_in, dw_out, dw_in,
-    text_part, text_in, text_all, gain_seq, gain_fsdp, send, recv, local_sems,
+    text_part, text_pair, text_sum, text_in, text_all, gain_seq, gain_fsdp, send, recv, local_sems,
 ):
     xl, y, xh, z, core = where()
     own = (xh * 4 + z) * 2 + core
@@ -304,13 +304,17 @@
         copies.make(gain_fsdp.at[group], gain_fsdp.at[group], fsdp_id(fsdp_peer(o)))
         for o in FSDP_OFFSETS
     ]
+    other_pair = {"seq_0": 1 - xh}
+    text_cross = copies.make(text_part.at[1 - xh], text_pair, other_pair)
     text_first, text_second = [], []
-    for o in FSDP_OFFSETS:
-        peer = seq_peer((o[0], o[1], 0))
-        to = {"seq_0": peer[0], "seq_1": peer[1]}
-        text_first.append(copies.make(text_part.at[peer[0], peer[1]], text_in.at[xh, z], to))
-        text_second.append(copies.make(text_all.at[core, xh, z], text_all.at[core, xh, z], to))
-    text_third = copies.make(text_all.at[core], text_all.at[core], other_core)
+    for d in range(1, 4):
+        at = (z + d) % 4
+        text_first.append(copies.make(text_sum.at[at], text_in.at[z], {"seq_1": at}))
+        text_second.append(
+            copies.make(text_all.at[core, xh, z], text_all.at[core, xh, z], {"seq_1": at})
+        )
+    text_third = copies.make(text_all.at[core, xh], text_all.at[core, xh], other_pair)
+    text_fourth = copies.make(text_all.at[core], text_all.at[core], other_core)
 
     def dx_value(plane, d, h):
         start = (plane * 4 + d) * IMAGE_CHUNK + h * half
@@ -440,11 +444,11 @@
         t.down[1][h].wait_recv()
         shared[1, 1, h].start()
     project_unit(1, 0)
+    project_unit(1, 1)
+    project_unit(1, 3)
     for h in range(2):
         t.far[h].wait_recv()
         shared[1, 2, h].start()
-    project_unit(1, 1)
-    project_unit(1, 3)
     project_unit(1, 2)
 
     exponential_blocks(1, plane_keys(0) + plane_keys(1) + [IMAGE_ROWS])
@@ -524,33 +528,38 @@
             chunk(at * 2 + core), chunk(at)
         )
 
-    def weight_part(j):
+    def weight_parts(plane):
         block = 2 * WEIGHT_ROWS
-        dw[j * block : (j + 1) * block, :] = dot_tn(
-            tokens[:, j * block : (j + 1) * block], grads[...]
-        )
-
+        pair = xl if plane == 0 else 1 - xl
+        for j in range(2):
+            at = pl.ds(pl.multiple_of((pair * 2 + j) * block, block), block)
+            dw[at, :] = dot_tn(tokens[:, at], grads[...])
+
+    token_grads(IMAGE_ROWS, text_count)
+    text_shared.start()
     unit_grads(1, 1)
     unit_grads(1, 2)
-    token_grads(IMAGE_ROWS, text_count)
-    text_shared.start()
-    unit_grads(1, 3)
     weights_shared.wait_recv()
+    text_shared.wait_recv()
+    text_terms = input_part(text_share(core), text_got).astype(BF16)
+    rows, width = text_part.shape[2:]
+    for a, b in UNITS:
+        text_part[a, b] = text_terms[b * rows : (b + 1) * rows, a * width : (a + 1) * width]
+    text_cross.start()
     input_sum(1, 1)
     dx_ring.send_up()
+    unit_grads(1, 3)
     input_sum(1, 2)
     dx_ring.send_far()
+    unit_grads(0, 2)
     input_sum(1, 3)
     dx_ring.send_down()
-    text_shared.wait_recv()
-    text_sum = input_part(text_share(core), text_got).astype(BF16)
-    rows, width = text_part.shape[2:]
-    for a, b in UNITS:
-        text_part[a, b] = text_sum[b * rows : (b + 1) * rows, a * width : (a + 1) * width]
+    text_cross.wait_recv()
+    text_sum[...] = (text_part[xh].astype(F32) + text_pair[...].astype(F32)).astype(BF16)
     for copy in text_first:
         copy.start()
-    text_in[xh, z] = text_part[xh, z]
-    for unit in ((0, 2), (0, 1), (0, 3), (1, 0), (0, 0)):
+    text_in[z] = text_sum[z]
+    for unit in ((0, 1), (0, 3), (1, 0), (0, 0)):
         unit_grads(*unit)
     gain_seq[own] = jnp.zeros(gain_seq.shape[1:], F32)
     gain_seq[own, 0:1, :] = jnp.sum(gsum[0:8, :], axis=0, keepdims=True)
@@ -559,48 +568,48 @@
         copy.start()
     input_sum(0, 2)
     dx_ring.own_far(0)
-    weight_part(0)
-    weight_part(1)
+    weight_parts(1)
+    dw_ring.first(1)
     input_sum(0, 1)
     dx_ring.own_up()
     dx_ring.own_far(1)
     input_sum(0, 3)
     dx_ring.own_down()
-    weight_part(2)
-    weight_part(3)
-    dw_ring.first(1)
+    for copy in text_first:
+        copy.wait_recv()
+    text_all[core, xh, z] = jnp.sum(text_in[...].astype(F32), axis=0).astype(BF16)
+    for copy in text_second:
+        copy.start()
     input_sum(1, 0)
     dx_ring.cross()
+    weight_parts(0)
+    dw_ring.pass_on(1)
     dw_ring.first(0)
     dx_ring.pass_on(0)
-    for copy in text_first:
-        copy.wait_recv()
-    text_all[core, xh, z] = jnp.sum(text_in[...].astype(F32), axis=(0, 1)).astype(BF16)
-    for copy in text_second:
-        copy.start()
-    dw_ring.pass_on(1)
     for copy in gain_first:
         copy.wait_recv()
     gain_fsdp[group] = jnp.sum(gain_seq[...], axis=0)
     for copy in gain_second:
         copy.start()
+    dw_ring.cross()
     dx_ring.pass_on(1)
+    for copy in text_second:
+        copy.wait_recv()
+    text_third.start()
+    input_sum(0, 0)
     dw_ring.pass_on(0)
-    dw_ring.cross()
-    input_sum(0, 0)
     for copy in gain_second:
         copy.wait_recv()
     gain_out[...] = jnp.sum(gain_fsdp[...], axis=0)[0:2]
-    for copy in text_second:
-        copy.wait_recv()
-    text_third.start()
+    text_third.wait_recv()
+    text_fourth.start()
     for h in range(2):
         image_out[h * half : (h + 1) * half, :] = dx_ring.total(h).astype(BF16)
     for h in range(2):
         total = dw_ring.total(h)
         for j in range(3):
             weight_out[j, h * whalf : (h + 1) * whalf, :] = total[:, j * HEAD : (j + 1) * HEAD]
-    text_third.wait_recv()
+    text_fourth.wait_recv()
     for c in range(2):
         for a, b in UNITS:
             text_out[
@@ -622,7 +631,7 @@
     text_piece = (2, 4, text_count // 8, features // 2)
     n_copies = (
         2 * GATHER_COPIES + 16 + len(SEQ_OFFSETS) + 1 + 9
-        + len(SEQ_OFFSETS) + len(FSDP_OFFSETS) + 2 * len(FSDP_OFFSETS) + 1 + 2 * REDUCE_COPIES
+        + len(SEQ_OFFSETS) + len(FSDP_OFFSETS) + 1 + 2 * 3 + 2 + 2 * REDUCE_COPIES
     )
     return pl.pallas_call(
         step_kernel,
@@ -656,7 +665,9 @@
             pltpu.VMEM((REDUCE_COPIES, whalf, WIDTH), BF16),
             pltpu.VMEM((REDUCE_COPIES, whalf, WIDTH), BF16),
             pltpu.VMEM(text_piece, BF16),
-            pltpu.VMEM(text_piece, BF16),
+            pltpu.VMEM(text_piece[1:], BF16),
+            pltpu.VMEM(text_piece[1:], BF16),
+            pltpu.VMEM(text_piece[1:], BF16),
             pltpu.VMEM((2, *text_piece), BF16),
             pltpu.VMEM((16, 8, HEAD), F32),
             pltpu.VMEM((8, 8, HEAD), F32),

time: 96.9 us -> 96.4 us (level)
  no operation moved by 1% of the time
where the time goes in v7:
time: 96.4 us; the launch traced here: 96 us
  Pallas kernels  95.2 us (99%)
    pallas_call x1, Pallas kernels, step(): pl.pallas_call(step_kernel, out_shape=(jax.ShapeDtypeStruct((IMAGE_CHUNK,...  93.2 us
    pallas_call x1, Pallas kernels, store(): pl.pallas_call(store_kernel, out_shape=tuple((jax.ShapeDtypeStruct(a.shap...  2.04 us

profile of v7, /device:TPU:1, one launch (start us, length us, event | category | flops | bytes accessed | tf_op | source)
XLA Modules:
  0.0 96.0 jit_solution(11978755582049798422)
XLA Ops:
  0.6 93.2 %step.1 = (bf16[128,1536]{1,0:T(8,128)(2,1)}, bf16[128,1536]{1,0:T(8,128)(2,1)}, f32[3,192,128]{2,1,0:T(8,128)}, f32[2,128]{1,0:T(2,128)}) custom-call(bf16[128,1536]{1,0:T(8,128)(2,1)} %bitcast.13, bf16[128,1536]{1,0:T(8,128)(2,1)} %bitcast.14, bf16[3,192,2048]{2,1,0:T(8,128)(2,1)} %bitcast.10, f32[1,128]{1,0:T(1,128)} %bitcast.15, f32[1,128]{1,0:T(1,128)} %bitcast.16, ...), custom_call_target="tpu_custom_call" | custom-call | tf_op jit(solution)/shard_map/step/pallas_call | solution.py:636
  93.8 2.0 %store.1 = (bf16[128,1536]{1,0:T(8,128)(2,1)}, bf16[128,1536]{1,0:T(8,128)(2,1)}, f32[3,192,128]{2,1,0:T(8,128)}, f32[2,128]{1,0:T(2,128)}) custom-call(bf16[128,1536]{1,0:T(8,128)(2,1)} %get-tuple-element.12.refs_0_, bf16[128,1536]{1,0:T(8,128)(2,1)} %get-tuple-element.13.refs_1_, f32[3,192,128]{2,1,0:T(8,128)} %get-tuple-element.14.refs_2_, ...), custom_call_target="tpu_custom_call" | custom-call | tf_op jit(solution)/shard_map/store/pallas_call | solution.py:702

commit v8 on v7

--- a/solution.py
+++ b/solution.py
@@ -130,9 +130,8 @@
         self.pieces[i].wait_recv()
         return self.arrived[i].astype(F32)
 
-    def send_far(self):
-        self.put(0, self.value(1, 2, 0))
-        self.put(1, self.value(1, 2, 1))
+    def send_far(self, h):
+        self.put(h, self.value(1, 2, h))
 
     def send_up(self):
         self.put(2, self.value(1, 1, 0))
@@ -310,11 +309,16 @@
     for d in range(1, 4):
         at = (z + d) % 4
         text_first.append(copies.make(text_sum.at[at], text_in.at[z], {"seq_1": at}))
+    for o in FSDP_OFFSETS:
+        peer = seq_peer((o[0], o[1], 0))
         text_second.append(
-            copies.make(text_all.at[core, xh, z], text_all.at[core, xh, z], {"seq_1": at})
+            copies.make(
+                text_all.at[core, xh, z],
+                text_all.at[core, xh, z],
+                {"seq_0": peer[0], "seq_1": peer[1]},
+            )
         )
-    text_third = copies.make(text_all.at[core, xh], text_all.at[core, xh], other_pair)
-    text_fourth = copies.make(text_all.at[core], text_all.at[core], other_core)
+    text_third = copies.make(text_all.at[core], text_all.at[core], other_core)
 
     def dx_value(plane, d, h):
         start = (plane * 4 + d) * IMAGE_CHUNK + h * half
@@ -535,32 +539,35 @@
             at = pl.ds(pl.multiple_of((pair * 2 + j) * block, block), block)
             dw[at, :] = dot_tn(tokens[:, at], grads[...])
 
-    token_grads(IMAGE_ROWS, text_count)
-    text_shared.start()
     unit_grads(1, 1)
     unit_grads(1, 2)
     weights_shared.wait_recv()
+    input_sum(1, 1)
+    dx_ring.send_up()
+    input_sum(1, 2)
+    dx_ring.send_far(0)
+    unit_grads(1, 3)
+    token_grads(IMAGE_ROWS, text_count)
+    text_shared.start()
+    input_sum(1, 3)
+    dx_ring.send_down()
     text_shared.wait_recv()
     text_terms = input_part(text_share(core), text_got).astype(BF16)
     rows, width = text_part.shape[2:]
     for a, b in UNITS:
         text_part[a, b] = text_terms[b * rows : (b + 1) * rows, a * width : (a + 1) * width]
     text_cross.start()
-    input_sum(1, 1)
-    dx_ring.send_up()
-    unit_grads(1, 3)
-    input_sum(1, 2)
-    dx_ring.send_far()
+    dx_ring.send_far(1)
     unit_grads(0, 2)
-    input_sum(1, 3)
-    dx_ring.send_down()
+    unit_grads(0, 1)
+    unit_grads(0, 3)
     text_cross.wait_recv()
     text_sum[...] = (text_part[xh].astype(F32) + text_pair[...].astype(F32)).astype(BF16)
     for copy in text_first:
         copy.start()
     text_in[z] = text_sum[z]
-    for unit in ((0, 1), (0, 3), (1, 0), (0, 0)):
-        unit_grads(*unit)
+    unit_grads(1, 0)
+    unit_grads(0, 0)
     gain_seq[own] = jnp.zeros(gain_seq.shape[1:], F32)
     gain_seq[own, 0:1, :] = jnp.sum(gsum[0:8, :], axis=0, keepdims=True)
     gain_seq[own, 1:2, :] = jnp.sum(gsum[8:16, :], axis=0, keepdims=True)
@@ -593,23 +600,21 @@
         copy.start()
     dw_ring.cross()
     dx_ring.pass_on(1)
+    input_sum(0, 0)
     for copy in text_second:
         copy.wait_recv()
     text_third.start()
-    input_sum(0, 0)
     dw_ring.pass_on(0)
     for copy in gain_second:
         copy.wait_recv()
     gain_out[...] = jnp.sum(gain_fsdp[...], axis=0)[0:2]
-    text_third.wait_recv()
-    text_fourth.start()
     for h in range(2):
         image_out[h * half : (h + 1) * half, :] = dx_ring.total(h).astype(BF16)
     for h in range(2):
         total = dw_ring.total(h)
         for j in range(3):
             weight_out[j, h * whalf : (h + 1) * whalf, :] = total[:, j * HEAD : (j + 1) * HEAD]
-    text_fourth.wait_recv()
+    text_third.wait_recv()
     for c in range(2):
         for a, b in UNITS:
             text_out[
@@ -631,7 +636,7 @@
     text_piece = (2, 4, text_count // 8, features // 2)
     n_copies = (
         2 * GATHER_COPIES + 16 + len(SEQ_OFFSETS) + 1 + 9
-        + len(SEQ_OFFSETS) + len(FSDP_OFFSETS) + 1 + 2 * 3 + 2 + 2 * REDUCE_COPIES
+        + len(SEQ_OFFSETS) + len(FSDP_OFFSETS) + 1 + 3 + len(FSDP_OFFSETS) + 1 + 2 * REDUCE_COPIES
     )
     return pl.pallas_call(
         step_kernel,

time: 96.4 us -> 95.1 us (0.987)
  Pallas kernels: 95.2 us -> 93 us
    pallas_call x1, Pallas kernels: 93.2 us -> 91 us  [step(): pl.pallas_call(step_kernel, out_shape=(jax.ShapeDtypeStruct((IMAGE_CHUNK,...]
where the time goes in v8:
time: 95.1 us; the launch traced here: 93.8 us
  Pallas kernels  93 us (98%)
    pallas_call x1, Pallas kernels, step(): pl.pallas_call(step_kernel, out_shape=(jax.ShapeDtypeStruct((IMAGE_CHUNK,...  91 us
    pallas_call x1, Pallas kernels, store(): pl.pallas_call(store_kernel, out_shape=tuple((jax.ShapeDtypeStruct(a.shap...  2.04 us

profile of v8, /device:TPU:1, one launch (start us, length us, event | category | flops | bytes accessed | tf_op | source)
XLA Modules:
  0.0 93.8 jit_solution(3003960859575065246)
XLA Ops:
  0.6 91.0 %step.1 = (bf16[128,1536]{1,0:T(8,128)(2,1)}, bf16[128,1536]{1,0:T(8,128)(2,1)}, f32[3,192,128]{2,1,0:T(8,128)}, f32[2,128]{1,0:T(2,128)}) custom-call(bf16[128,1536]{1,0:T(8,128)(2,1)} %bitcast.13, bf16[128,1536]{1,0:T(8,128)(2,1)} %bitcast.14, bf16[3,192,2048]{2,1,0:T(8,128)(2,1)} %bitcast.10, f32[1,128]{1,0:T(1,128)} %bitcast.15, f32[1,128]{1,0:T(1,128)} %bitcast.16, ...), custom_call_target="tpu_custom_call" | custom-call | tf_op jit(solution)/shard_map/step/pallas_call | solution.py:641
  91.6 2.0 %store.1 = (bf16[128,1536]{1,0:T(8,128)(2,1)}, bf16[128,1536]{1,0:T(8,128)(2,1)}, f32[3,192,128]{2,1,0:T(8,128)}, f32[2,128]{1,0:T(2,128)}) custom-call(bf16[128,1536]{1,0:T(8,128)(2,1)} %get-tuple-element.12.refs_0_, bf16[128,1536]{1,0:T(8,128)(2,1)} %get-tuple-element.13.refs_1_, f32[3,192,128]{2,1,0:T(8,128)} %get-tuple-element.14.refs_2_, ...), custom_call_target="tpu_custom_call" | custom-call | tf_op jit(solution)/shard_map/store/pallas_call | solution.py:707

commit v9 on v8

--- a/solution.py
+++ b/solution.py
@@ -130,8 +130,9 @@
         self.pieces[i].wait_recv()
         return self.arrived[i].astype(F32)
 
-    def send_far(self, h):
-        self.put(h, self.value(1, 2, h))
+    def send_far(self):
+        self.put(0, self.value(1, 2, 0))
+        self.put(1, self.value(1, 2, 1))
 
     def send_up(self):
         self.put(2, self.value(1, 1, 0))
@@ -379,8 +380,6 @@
     t.pass_down[0].wait_recv()
     t.far[1].start()
     shared[0, 2, 1].start()
-    for copy in exchanged:
-        copy.start()
     for plane in range(2):
         w.up[plane][1].wait_recv()
         w.down[plane][0].wait_recv()
@@ -447,6 +446,8 @@
         shared[1, 3, h].start()
         t.down[1][h].wait_recv()
         shared[1, 1, h].start()
+    for copy in exchanged:
+        copy.start()
     project_unit(1, 0)
     project_unit(1, 1)
     project_unit(1, 3)
@@ -540,32 +541,30 @@
             dw[at, :] = dot_tn(tokens[:, at], grads[...])
 
     unit_grads(1, 1)
+    unit_grads(1, 3)
     unit_grads(1, 2)
     weights_shared.wait_recv()
     input_sum(1, 1)
     dx_ring.send_up()
+    input_sum(1, 3)
+    dx_ring.send_down()
     input_sum(1, 2)
-    dx_ring.send_far(0)
-    unit_grads(1, 3)
+    dx_ring.send_far()
+    unit_grads(0, 1)
     token_grads(IMAGE_ROWS, text_count)
     text_shared.start()
-    input_sum(1, 3)
-    dx_ring.send_down()
+    input_sum(0, 1)
+    dx_ring.own_up()
+    unit_grads(0, 3)
     text_shared.wait_recv()
     text_terms = input_part(text_share(core), text_got).astype(BF16)
     rows, width = text_part.shape[2:]
     for a, b in UNITS:
         text_part[a, b] = text_terms[b * rows : (b + 1) * rows, a * width : (a + 1) * width]
     text_cross.start()
-    dx_ring.send_far(1)
+    input_sum(0, 3)
+    dx_ring.own_down()
     unit_grads(0, 2)
-    unit_grads(0, 1)
-    unit_grads(0, 3)
-    text_cross.wait_recv()
-    text_sum[...] = (text_part[xh].astype(F32) + text_pair[...].astype(F32)).astype(BF16)
-    for copy in text_first:
-        copy.start()
-    text_in[z] = text_sum[z]
     unit_grads(1, 0)
     unit_grads(0, 0)
     gain_seq[own] = jnp.zeros(gain_seq.shape[1:], F32)
@@ -573,41 +572,42 @@
     gain_seq[own, 1:2, :] = jnp.sum(gsum[8:16, :], axis=0, keepdims=True)
     for copy in gain_first:
         copy.start()
+    weight_parts(1)
+    dw_ring.first(1)
     input_sum(0, 2)
     dx_ring.own_far(0)
-    weight_parts(1)
-    dw_ring.first(1)
-    input_sum(0, 1)
-    dx_ring.own_up()
     dx_ring.own_far(1)
-    input_sum(0, 3)
-    dx_ring.own_down()
+    text_cross.wait_recv()
+    text_sum[...] = (text_part[xh].astype(F32) + text_pair[...].astype(F32)).astype(BF16)
     for copy in text_first:
-        copy.wait_recv()
-    text_all[core, xh, z] = jnp.sum(text_in[...].astype(F32), axis=0).astype(BF16)
-    for copy in text_second:
         copy.start()
+    text_in[z] = text_sum[z]
     input_sum(1, 0)
     dx_ring.cross()
     weight_parts(0)
     dw_ring.pass_on(1)
     dw_ring.first(0)
     dx_ring.pass_on(0)
+    dx_ring.pass_on(1)
+    for copy in text_first:
+        copy.wait_recv()
+    text_all[core, xh, z] = jnp.sum(text_in[...].astype(F32), axis=0).astype(BF16)
+    for copy in text_second:
+        copy.start()
+    dw_ring.cross()
     for copy in gain_first:
         copy.wait_recv()
     gain_fsdp[group] = jnp.sum(gain_seq[...], axis=0)
     for copy in gain_second:
         copy.start()
-    dw_ring.cross()
-    dx_ring.pass_on(1)
     input_sum(0, 0)
-    for copy in text_second:
-        copy.wait_recv()
-    text_third.start()
     dw_ring.pass_on(0)
     for copy in gain_second:
         copy.wait_recv()
     gain_out[...] = jnp.sum(gain_fsdp[...], axis=0)[0:2]
+    for copy in text_second:
+        copy.wait_recv()
+    text_third.start()
     for h in range(2):
         image_out[h * half : (h + 1) * half, :] = dx_ring.total(h).astype(BF16)
     for h in range(2):

time: 95.1 us -> 97.4 us (1.024); the launches traced: 93.8 us -> 97.3 us
  Pallas kernels: 93 us -> 96.5 us
    pallas_call x1, Pallas kernels: 91 us -> 94.4 us  [step(): pl.pallas_call(step_kernel, out_shape=(jax.ShapeDtypeStruct((IMAGE_CHUNK,...]
where the time goes in v9:
time: 97.4 us; the launch traced here: 97.3 us
  Pallas kernels  96.5 us (99%)
    pallas_call x1, Pallas kernels, step(): pl.pallas_call(step_kernel, out_shape=(jax.ShapeDtypeStruct((IMAGE_CHUNK,...  94.4 us
    pallas_call x1, Pallas kernels, store(): pl.pallas_call(store_kernel, out_shape=tuple((jax.ShapeDtypeStruct(a.shap...  2.04 us

profile of v9, /device:TPU:1, one launch (start us, length us, event | category | flops | bytes accessed | tf_op | source)
XLA Modules:
  0.0 97.3 jit_solution(15265410703530039934)
XLA Ops:
  0.6 94.4 %step.1 = (bf16[128,1536]{1,0:T(8,128)(2,1)}, bf16[128,1536]{1,0:T(8,128)(2,1)}, f32[3,192,128]{2,1,0:T(8,128)}, f32[2,128]{1,0:T(2,128)}) custom-call(bf16[128,1536]{1,0:T(8,128)(2,1)} %bitcast.13, bf16[128,1536]{1,0:T(8,128)(2,1)} %bitcast.14, bf16[3,192,2048]{2,1,0:T(8,128)(2,1)} %bitcast.10, f32[1,128]{1,0:T(1,128)} %bitcast.15, f32[1,128]{1,0:T(1,128)} %bitcast.16, ...), custom_call_target="tpu_custom_call" | custom-call | tf_op jit(solution)/shard_map/step/pallas_call | solution.py:641
  95.1 2.0 %store.1 = (bf16[128,1536]{1,0:T(8,128)(2,1)}, bf16[128,1536]{1,0:T(8,128)(2,1)}, f32[3,192,128]{2,1,0:T(8,128)}, f32[2,128]{1,0:T(2,128)}) custom-call(bf16[128,1536]{1,0:T(8,128)(2,1)} %get-tuple-element.12.refs_0_, bf16[128,1536]{1,0:T(8,128)(2,1)} %get-tuple-element.13.refs_1_, f32[3,192,128]{2,1,0:T(8,128)} %get-tuple-element.14.refs_2_, ...), custom_call_target="tpu_custom_call" | custom-call | tf_op jit(solution)/shard_map/store/pallas_call | solution.py:707

commit v10 on v8

--- a/solution.py
+++ b/solution.py
@@ -379,8 +379,6 @@
     t.pass_down[0].wait_recv()
     t.far[1].start()
     shared[0, 2, 1].start()
-    for copy in exchanged:
-        copy.start()
     for plane in range(2):
         w.up[plane][1].wait_recv()
         w.down[plane][0].wait_recv()
@@ -447,6 +445,8 @@
         shared[1, 3, h].start()
         t.down[1][h].wait_recv()
         shared[1, 1, h].start()
+    for copy in exchanged:
+        copy.start()
     project_unit(1, 0)
     project_unit(1, 1)
     project_unit(1, 3)
@@ -547,10 +547,10 @@
     input_sum(1, 2)
     dx_ring.send_far(0)
     unit_grads(1, 3)
+    input_sum(1, 3)
+    dx_ring.send_down()
     token_grads(IMAGE_ROWS, text_count)
     text_shared.start()
-    input_sum(1, 3)
-    dx_ring.send_down()
     text_shared.wait_recv()
     text_terms = input_part(text_share(core), text_got).astype(BF16)
     rows, width = text_part.shape[2:]

time: 95.1 us -> 96 us (level)
  no operation moved by 1% of the time
where the time goes in v10:
time: 96 us; the launch traced here: 94.7 us
  Pallas kernels  93.9 us (98%)
    pallas_call x1, Pallas kernels, step(): pl.pallas_call(step_kernel, out_shape=(jax.ShapeDtypeStruct((IMAGE_CHUNK,...  91.8 us
    pallas_call x1, Pallas kernels, store(): pl.pallas_call(store_kernel, out_shape=tuple((jax.ShapeDtypeStruct(a.shap...  2.04 us

profile of v10, /device:TPU:1, one launch (start us, length us, event | category | flops | bytes accessed | tf_op | source)
XLA Modules:
  0.0 94.7 jit_solution(16758344683258252548)
XLA Ops:
  0.6 91.8 %step.1 = (bf16[128,1536]{1,0:T(8,128)(2,1)}, bf16[128,1536]{1,0:T(8,128)(2,1)}, f32[3,192,128]{2,1,0:T(8,128)}, f32[2,128]{1,0:T(2,128)}) custom-call(bf16[128,1536]{1,0:T(8,128)(2,1)} %bitcast.13, bf16[128,1536]{1,0:T(8,128)(2,1)} %bitcast.14, bf16[3,192,2048]{2,1,0:T(8,128)(2,1)} %bitcast.10, f32[1,128]{1,0:T(1,128)} %bitcast.15, f32[1,128]{1,0:T(1,128)} %bitcast.16, ...), custom_call_target="tpu_custom_call" | custom-call | tf_op jit(solution)/shard_map/step/pallas_call | solution.py:641
  92.5 2.0 %store.1 = (bf16[128,1536]{1,0:T(8,128)(2,1)}, bf16[128,1536]{1,0:T(8,128)(2,1)}, f32[3,192,128]{2,1,0:T(8,128)}, f32[2,128]{1,0:T(2,128)}) custom-call(bf16[128,1536]{1,0:T(8,128)(2,1)} %get-tuple-element.12.refs_0_, bf16[128,1536]{1,0:T(8,128)(2,1)} %get-tuple-element.13.refs_1_, f32[3,192,128]{2,1,0:T(8,128)} %get-tuple-element.14.refs_2_, ...), custom_call_target="tpu_custom_call" | custom-call | tf_op jit(solution)/shard_map/store/pallas_call | solution.py:707
